TPU v7x, 32 devices: a whole 2x2x4 slice. The times are simulated.
32 devices in a mesh: inter: 16 (over z, y, core), intra: 2 (over x).
Axes of the slice: x: 2, y: 2, z: 4, core: 2. Of those that a mesh axis runs over, the one named last changes fastest.
Arguments:
- partials: bfloat16 [32, 16, 5120], P(('inter', 'intra')), may hold values from -6 to 6
- scales: bfloat16 [32, 16, 20], P(('inter', 'intra')), may hold values from 64 to 1024
- overflow_pos: int32 [32, 1], P(('inter', 'intra')), may hold values from -81920 to 81919, as said below
- weights: float32 [16, 5120], P('inter', 'intra'), may hold values from -6 to 6
- exponent: int32 [], replicated, may hold values from 10 to 16
Outputs:
- grad_out: float32 [16, 5120], P('inter', 'intra')
- block_scale: float32 [16, 20], P('inter', 'intra')
- master_out: float32 [16, 5120], P('inter', 'intra')
- new_exponent: int32 [], replicated
- overflow_count: int32 [], replicated
Inputs may be any that keep to these rules, and one draw needn't show every extreme that they name: `overflow_pos`: A negative entry means no overflow on that device; otherwise it is the flat position (row times 5120 plus column) of an overflowed value of that device's partial.
All inputs are finite; a program needn't handle non-finite values.
Results may differ from a plain program's by a relative error of at most 0.0005.
Values may be sent and summed in bfloat16 or wider, within the bound.
A program may use at most 64 MiB of HBM per device.

v0:
```python
import functools

import jax
import jax.numpy as jnp
from jax import lax
from jax.experimental import pallas as pl
from jax.experimental.pallas import tpu as pltpu
from jax.sharding import PartitionSpec as P

LANES = 128
ROW_GROUP = 16
SOURCE_GROUP = 32


def exchange(inter_size, intra_size, block_len, x_hbm, s_hbm, pos_hbm, w_hbm, e_hbm,
             grad_ref, scale_ref, master_ref, whole_ref,
             xv, sv, pos_ref, w_ref, e_ref, staged, outgoing, incoming,
             load_sems, own_sem, send_sem, recv_sem):
    total = inter_size * intra_size
    row_total, full_width = xv.shape
    block_total = sv.shape[1]
    share_cols = full_width // intra_size
    half = share_cols // 2
    tiles = half // LANES
    my_inter = lax.axis_index("inter")
    my_intra = lax.axis_index("intra")
    me = my_inter * intra_size + my_intra

    loads = [
        pltpu.make_async_copy(src, dst, load_sems.at[n])
        for n, (src, dst) in enumerate(
            ((x_hbm.at[0], xv), (s_hbm.at[0], sv), (pos_hbm, pos_ref), (w_hbm, w_ref), (e_hbm, e_ref))
        )
    ]
    for load in loads:
        load.start()

    barrier = pltpu.get_barrier_semaphore()
    paired = total & (total - 1) == 0 and False
    flips = [bit * (1 - 2 * lax.rem(me // bit, 2)) for bit in (2**n for n in range(total.bit_length() - 1))]

    def peer(k):
        if paired:
            target = me + sum(flip for n, flip in enumerate(flips) if k >> n & 1)
        else:
            target = lax.rem(me + k, total)
        return target // intra_size, lax.rem(target, intra_size)

    def each_peer(visit):
        if paired:
            for k in reversed(range(1, total)):
                visit(k)
        else:
            lax.fori_loop(1, total, lambda k, carry: (visit(k), carry)[1], 0)

    def greet(target):
        pl.semaphore_signal(barrier, inc=1, device_id=(target // intra_size, target % intra_size), device_id_type=pl.DeviceIdType.MESH)

    if True:
        for n in range(total):
            greet(n)

    for load in loads[:3]:
        load.wait()
    flag = jnp.where(pos_ref[0, 0] >= 0, jnp.float32(1), jnp.float32(0))
    lane = lax.broadcasted_iota(jnp.int32, (ROW_GROUP, LANES), 1)
    pick_block = lax.broadcasted_iota(jnp.int32, (block_total, LANES), 0)
    pick_lane = lax.broadcasted_iota(jnp.int32, (block_total, LANES), 1)

    def stage(group, carry):
        first = pl.multiple_of(group * ROW_GROUP, ROW_GROUP)
        rows = pl.ds(first, ROW_GROUP)
        scale_rows = sv[rows, :]
        for b in range(intra_size):
            for h in range(2):
                start = (b * 2 + h) * half
                staged[:, b, h, pl.ds(0, half)] = xv[rows, pl.ds(start, half)].astype(jnp.float32)
                hit = (pick_block == (start + pick_lane * LANES) // block_len) & (pick_lane < tiles)
                spread = jnp.dot(scale_rows, hit.astype(jnp.float32).astype(jnp.bfloat16),
                                 preferred_element_type=jnp.float32)
                staged[:, b, h, pl.ds(half, LANES)] = jnp.where(lane == tiles, flag, spread)
        outgoing[rows] = staged[...].astype(jnp.bfloat16)
        return carry

    if True:
        lax.fori_loop(0, row_total // ROW_GROUP, stage, 0)

    own = pltpu.make_async_copy(outgoing.at[my_inter, my_intra], incoming.at[me], own_sem)
    own.start()
    if True:
        pl.semaphore_wait(barrier, total)

    def send(target):
        to_inter, to_intra = target // intra_size, target % intra_size
        pltpu.make_async_remote_copy(
            src_ref=outgoing.at[to_inter, to_intra],
            dst_ref=incoming.at[me],
            send_sem=send_sem,
            recv_sem=recv_sem,
            device_id=(to_inter, to_intra),
            device_id_type=pl.DeviceIdType.MESH,
        ).start()

    if True:
        for n in range(total - 1):
            send(n + (n >= me).astype(jnp.int32))
    for load in loads[3:]:
        load.wait()
    exponent = e_ref[0]
    unscale = jnp.exp2(jnp.full((1, LANES), -exponent.astype(jnp.float32), jnp.float32))
    own.wait()
    others = incoming.at[pl.ds(0, total - 1)]
    if True:
        pltpu.make_async_copy(others, others, recv_sem).wait()

    def reduce(group, sums):
        sources = pl.ds(group * SOURCE_GROUP, SOURCE_GROUP)
        factors = incoming[sources, :, pl.ds(half, LANES)].astype(jnp.float32)
        added = [
            jnp.sum(incoming[sources, :, pl.ds(t * LANES, LANES)].astype(jnp.float32) * factors[:, :, t:t + 1], axis=0)
            for t in range(tiles)
        ]
        added.append(jnp.sum(factors, axis=0))
        return tuple(s + a for s, a in zip(sums, added))

    sums = tuple(jnp.zeros((2, LANES), jnp.float32) for _ in range(tiles + 1))
    if True:
        if total == SOURCE_GROUP:
            sums = reduce(0, sums)
        else:
            sums = lax.fori_loop(0, total // SOURCE_GROUP, reduce, sums)
    lane = lax.broadcasted_iota(jnp.int32, (1, LANES), 1)
    count = jnp.sum(jnp.where(lane == tiles, sums[tiles][0:1], 0.0)).astype(jnp.int32)
    blocks = share_cols // block_len
    per_block = block_len // LANES
    block_lane = lax.broadcasted_iota(jnp.int32, (1, blocks), 1)
    largest = jnp.zeros((1, blocks), jnp.float32)
    tops = []
    for h in range(2):
        for t in range(tiles):
            grad = sums[t][h:h + 1] * unscale
            columns = pl.ds(h * half + t * LANES, LANES)
            grad_ref[0:1, columns] = grad
            weights = w_ref[0:1, columns]
            master_ref[0:1, columns] = jnp.where(count == 0, weights - 0.5 * grad, weights)
            tops.append(jnp.abs(grad))
    for n in range(blocks):
        top = functools.reduce(jnp.maximum, tops[n * per_block:(n + 1) * per_block])
        largest = jnp.where(block_lane == n, jnp.max(top, axis=1, keepdims=True), largest)
    scale_ref[...] = largest / 127.0
    whole_ref[0:1, pl.ds(0, LANES)] = jnp.full((1, LANES), exponent - jnp.where(count > 0, 1, 0), jnp.int32)
    whole_ref[0:1, pl.ds(LANES, LANES)] = jnp.full((1, LANES), count, jnp.int32)
    if True:
        pltpu.make_async_copy(others, others, send_sem).wait()


def finish(grad_in, scale_in, master_in, whole_in, grad_ref, scale_ref, master_ref, exp_ref, count_ref, sems):
    copies = [
        pltpu.make_async_copy(src, dst, sems.at[n])
        for n, (src, dst) in enumerate(((grad_in, grad_ref), (scale_in, scale_ref), (master_in, master_ref)))
    ]
    for copy in copies:
        copy.start()
    exp_ref[0] = whole_in[0:1, 0:1][0, 0]
    count_ref[0] = whole_in[0:1, LANES:LANES + 1][0, 0]
    for copy in copies:
        copy.wait()


def on_device(partials, scales, overflow_pos, weights, exponent):
    inter_size = lax.axis_size("inter")
    intra_size = lax.axis_size("intra")
    total = inter_size * intra_size
    row_total, full_width = partials.shape[1], partials.shape[2]
    block_total = scales.shape[2]
    block_len = full_width // block_total
    share_cols = full_width // intra_size
    blocks = share_cols // block_len
    width = share_cols // 2 + LANES
    any_space = pl.BlockSpec(memory_space=pl.ANY)
    vmem = pl.BlockSpec(memory_space=pltpu.VMEM)
    smem = pl.BlockSpec(memory_space=pltpu.SMEM)
    results = pl.pallas_call(
        functools.partial(exchange, inter_size, intra_size, block_len),
        out_shape=(
            pltpu.VMEM((1, share_cols), jnp.float32),
            pltpu.VMEM((1, blocks), jnp.float32),
            pltpu.VMEM((1, share_cols), jnp.float32),
            pltpu.VMEM((1, 2 * LANES), jnp.int32),
        ),
        in_specs=[any_space] * 5,
        out_specs=(vmem, vmem, vmem, vmem),
        scratch_shapes=[
            pltpu.VMEM((row_total, full_width), jnp.bfloat16),
            pltpu.VMEM((row_total, block_total), jnp.bfloat16),
            pltpu.SMEM((1, 1), jnp.int32),
            pltpu.VMEM((1, share_cols), jnp.float32),
            pltpu.SMEM((1,), jnp.int32),
            pltpu.VMEM((ROW_GROUP, intra_size, 2, width), jnp.float32),
            pltpu.VMEM((row_total, intra_size, 2, width), jnp.bfloat16),
            pltpu.VMEM((total, 2, width), jnp.bfloat16),
            pltpu.SemaphoreType.DMA((5,)),
            pltpu.SemaphoreType.DMA,
            pltpu.SemaphoreType.DMA,
            pltpu.SemaphoreType.DMA,
        ],
        compiler_params=pltpu.CompilerParams(collective_id=0, has_side_effects=True),
        name="exchange",
    )(partials, scales, overflow_pos, weights, exponent.reshape(1))
    grad_out, block_scale, master_out, new_exponent, count = pl.pallas_call(
        finish,
        out_shape=(
            jax.ShapeDtypeStruct((1, share_cols), jnp.float32),
            jax.ShapeDtypeStruct((1, blocks), jnp.float32),
            jax.ShapeDtypeStruct((1, share_cols), jnp.float32),
            jax.ShapeDtypeStruct((1,), jnp.int32),
            jax.ShapeDtypeStruct((1,), jnp.int32),
        ),
        in_specs=[vmem] * 4,
        out_specs=(any_space, any_space, any_space, smem, smem),
        scratch_shapes=[pltpu.SemaphoreType.DMA((3,))],
        name="finish",
    )(*(pltpu.with_memory_space_constraint(result, pltpu.VMEM) for result in results))
    return grad_out, block_scale, master_out, new_exponent.reshape(()), count.reshape(())


def solution(mesh):
    placed = (
        P(("inter", "intra"), None, None),
        P(("inter", "intra"), None, None),
        P(("inter", "intra"), None),
        P("inter", "intra"),
        P(),
    )
    return jax.shard_map(
        on_device,
        mesh=mesh,
        in_specs=placed,
        out_specs=(P("inter", "intra"), P("inter", "intra"), P("inter", "intra"), P(), P()),
        check_vma=False,
    )
```

profile of v0, /device:TPU:0, one launch (start us, length us, event | category | flops | bytes accessed | tf_op | source)
XLA Modules:
  0.0 14.0 jit_solution(4594579365459464275)
XLA Ops:
  1.9 10.9 %exchange.1 = (f32[1,2560]{1,0:T(1,128)S(1)}, f32[1,10]{1,0:T(1,128)S(1)}, f32[1,2560]{1,0:T(1,128)S(1)}, s32[1,256]{1,0:T(1,128)S(1)}) custom-call(bf16[1,16,5120]{2,1,0:T(8,128)(2,1)} %x_hbm.1, bf16[1,16,20]{2,1,0:T(8,128)(2,1)} %s_hbm.1, s32[1,1]{1,0:T(1,128)S(6)} %copy.10.pos_hbm, f32[1,2560]{1,0:T(1,128)} %w_hbm.1, s32[1]{0:T(128)} %bitcast.3.e_hbm), custom_call_target="tpu_custom_call" | custom-call | tf_op jit(solution)/shard_map/exchange/pallas_call | solution.py:183
  12.8 1.2 %finish.1 = (f32[1,2560]{1,0:T(1,128)}, f32[1,10]{1,0:T(1,128)}, f32[1,2560]{1,0:T(1,128)}, s32[1]{0:T(128)}, s32[1]{0:T(128)}) custom-call(f32[1,2560]{1,0:T(1,128)S(1)} %get-tuple-element.14.grad_in, f32[1,10]{1,0:T(1,128)S(1)} %get-tuple-element.15.scale_in, f32[1,2560]{1,0:T(1,128)S(1)} %get-tuple-element.16.master_in, ...), custom_call_target="tpu_custom_call" | custom-call | tf_op jit(solution)/shard_map/finish/pallas_call | solution.py:210
where the time goes:
time: 14.2 us; the launch traced here: 14 us
  Pallas kernels  12.1 us (85%)
  between operations  1.93 us (14%)
    pallas_call x1, Pallas kernels, on_device(): pl.pallas_call(functools.partial(exchange, inter_size, intra_size, block_...  10.9 us
    pallas_call x1, Pallas kernels, on_device(): pl.pallas_call(finish, out_shape=(jax.ShapeDtypeStruct((1, share_cols), j...  1.16 us

commit v1 on v0

v1 whole, which is shorter than its diff:
```python
import functools

import jax
import jax.numpy as jnp
from jax import lax
from jax.experimental import pallas as pl
from jax.experimental.pallas import tpu as pltpu
from jax.sharding import PartitionSpec as P

LANES = 128
CORES = 2
LINES = 2
MOST_LAYERS = 8
PREPARE_FLOPS = 60000000
ROW_GROUP = 16
SOURCE_GROUP = 32


def exchange(inter_size, intra_size, block_len, x_ref, tail_ref, meta_ref, w_hbm,
             grad_ref, scale_ref, master_ref, whole_ref,
             w_ref, staged, outgoing, incoming,
             load_sem, own_sem, send_sem, recv_sem, upper_sem):
    total = inter_size * intra_size
    xv = x_ref.at[0]
    row_total, full_width = xv.shape
    share_cols = full_width // intra_size
    half = share_cols // 2
    tiles = half // LANES
    my_inter = lax.axis_index("inter")
    my_intra = lax.axis_index("intra")
    me = my_inter * intra_size + my_intra

    barrier = pltpu.get_barrier_semaphore()
    cores, lines = CORES, LINES
    layers = inter_size // (cores * lines)
    ordered = layers * cores * lines == inter_size and layers <= MOST_LAYERS
    place = (my_inter // (cores * lines), lax.rem(my_inter // cores, lines), my_intra)
    ends = (layers, lines, intra_size)
    my_core = lax.rem(my_inter, cores)

    def each_chip(lows, highs, visit):
        def along_z(z, carry):
            def along_y(y, carry):
                def along_x(x, carry):
                    visit(z, y, x)
                    return carry
                return lax.fori_loop(lows[2], highs[2], along_x, carry)
            return lax.fori_loop(lows[1], highs[1], along_y, carry)
        lax.fori_loop(lows[0], highs[0], along_z, 0)

    def signal(semaphore, inter, intra):
        pl.semaphore_signal(semaphore, inc=1, device_id=(inter, intra), device_id_type=pl.DeviceIdType.MESH)

    if ordered:
        def greet(z, y, x):
            for core in range(cores):
                signal(barrier, (z * lines + y) * cores + core, x)

        if True:
            each_chip(place, ends, greet)
    else:
        for n in range(total):
            signal(barrier, n // intra_size, n % intra_size)

    load = pltpu.make_async_copy(w_hbm, w_ref, load_sem)
    load.start()

    def stage(group, carry):
        rows = pl.ds(pl.multiple_of(group * ROW_GROUP, ROW_GROUP), ROW_GROUP)
        for b in range(intra_size):
            for h in range(2):
                staged[:, b, h, :] = xv[rows, pl.ds((b * 2 + h) * half, half)].astype(jnp.float32)
        outgoing[rows, :, :, pl.ds(0, half)] = staged[...].astype(jnp.bfloat16)
        outgoing[rows, :, :, pl.ds(half, LANES)] = tail_ref[rows]
        return carry

    if True:
        lax.fori_loop(0, row_total // ROW_GROUP, stage, 0)

    own = pltpu.make_async_copy(outgoing.at[my_inter, my_intra], incoming.at[me], own_sem)
    own.start()

    def send(to_inter, to_intra):
        pltpu.make_async_remote_copy(
            src_ref=outgoing.at[to_inter, to_intra],
            dst_ref=incoming.at[me],
            send_sem=send_sem,
            recv_sem=recv_sem,
            device_id=(to_inter, to_intra),
            device_id_type=pl.DeviceIdType.MESH,
        ).start()

    if ordered:
        past = tuple(at + 1 for at in place)

        def send_chip(z, y, x):
            for core in range(cores):
                to_inter = (z * lines + y) * cores + core

                @pl.when((to_inter != my_inter) | (x != my_intra))
                def _():
                    send(to_inter, x)

        def tell(z, y, x):
            @pl.when((z != place[0]) | (y != place[1]) | (x != place[2]))
            def _():
                offset = ((place[0] - z) * lines + place[1] - y) * intra_size + place[2] - x
                signal(upper_sem.at[offset], (z * lines + y) * cores + my_core, x)

        if True:
            pl.semaphore_wait(barrier, past[0] * past[1] * past[2] * cores)
        if True:
            each_chip((0, 0, 0), past, tell)
        if True:
            each_chip((0, 0, 0), past, send_chip)
        offsets = [(dz, dy, dx) for dz in range(layers) for dy in range(lines) for dx in range(intra_size)]
        for offset in sorted(offsets, key=lambda at: (sum(at), at))[1:]:
            inside = functools.reduce(jnp.logical_and, [at + d < end for at, d, end in zip(place, offset, ends)])

            @pl.when(inside)
            def _():
                pl.semaphore_wait(upper_sem.at[(offset[0] * lines + offset[1]) * intra_size + offset[2]], 1)
                lows = tuple(at + d if d else 0 for at, d in zip(place, offset))
                highs = tuple(at + d + 1 for at, d in zip(place, offset))
                each_chip(lows, highs, send_chip)
    else:
        pl.semaphore_wait(barrier, total)
        for n in range(total - 1):
            target = n + (n >= me).astype(jnp.int32)
            send(target // intra_size, lax.rem(target, intra_size))
    load.wait()
    exponent = meta_ref[0:1, 1:2]
    unscale = jnp.exp2(jnp.broadcast_to(-exponent.astype(jnp.float32), (1, LANES)))
    own.wait()
    others = incoming.at[pl.ds(0, total - 1)]
    if True:
        pltpu.make_async_copy(others, others, recv_sem).wait()

    def reduce(group, sums):
        sources = pl.ds(group * SOURCE_GROUP, SOURCE_GROUP)
        factors = incoming[sources, :, pl.ds(half, LANES)].astype(jnp.float32)
        added = [
            jnp.sum(incoming[sources, :, pl.ds(t * LANES, LANES)].astype(jnp.float32) * factors[:, :, t:t + 1], axis=0)
            for t in range(tiles)
        ]
        added.append(jnp.sum(factors, axis=0))
        return tuple(s + a for s, a in zip(sums, added))

    sums = tuple(jnp.zeros((2, LANES), jnp.float32) for _ in range(tiles + 1))
    if True:
        if total == SOURCE_GROUP:
            sums = reduce(0, sums)
        else:
            sums = lax.fori_loop(0, total // SOURCE_GROUP, reduce, sums)
    lane = lax.broadcasted_iota(jnp.int32, (1, LANES), 1)
    count = jnp.sum(jnp.where(lane == tiles, sums[tiles][0:1], 0.0)).astype(jnp.int32)
    blocks = share_cols // block_len
    per_block = block_len // LANES
    block_lane = lax.broadcasted_iota(jnp.int32, (1, blocks), 1)
    largest = jnp.zeros((1, blocks), jnp.float32)
    tops = []
    for h in range(2):
        for t in range(tiles):
            grad = sums[t][h:h + 1] * unscale
            columns = pl.ds(h * half + t * LANES, LANES)
            grad_ref[0:1, columns] = grad
            weights = w_ref[0:1, columns]
            master_ref[0:1, columns] = jnp.where(count == 0, weights - 0.5 * grad, weights)
            tops.append(jnp.abs(grad))
    for n in range(blocks):
        top = functools.reduce(jnp.maximum, tops[n * per_block:(n + 1) * per_block])
        largest = jnp.where(block_lane == n, jnp.max(top, axis=1, keepdims=True), largest)
    scale_ref[...] = largest / 127.0
    whole_ref[0:1, pl.ds(0, LANES)] = jnp.broadcast_to(exponent - jnp.where(count > 0, 1, 0), (1, LANES))
    whole_ref[0:1, pl.ds(LANES, LANES)] = jnp.full((1, LANES), count, jnp.int32)
    if True:
        pltpu.make_async_copy(others, others, send_sem).wait()


def prepare(intra_size, half, block_len, meta_ref, s_ref, tail_ref):
    block_total = s_ref.shape[2]
    tiles = half // LANES
    row_total = s_ref.shape[1]
    flag = meta_ref[0:1, 0:1].astype(jnp.float32)
    lane = lax.broadcasted_iota(jnp.int32, (row_total, LANES), 1)
    pick_block = lax.broadcasted_iota(jnp.int32, (block_total, LANES), 0)
    pick_lane = lax.broadcasted_iota(jnp.int32, (block_total, LANES), 1)
    parts = []
    for b in range(intra_size):
        for h in range(2):
            start = (b * 2 + h) * half
            hit = (pick_block == (start + pick_lane * LANES) // block_len) & (pick_lane < tiles)
            spread = jnp.dot(s_ref[0], hit.astype(jnp.float32).astype(jnp.bfloat16),
                             preferred_element_type=jnp.float32)
            parts.append(jnp.where(lane == tiles, flag, spread))
    tail_ref[...] = jnp.stack(parts, axis=1).reshape(tail_ref.shape).astype(jnp.bfloat16)


def gather_scalars(pos_ref, exp_ref, meta_ref):
    lane = lax.broadcasted_iota(jnp.int32, (1, LANES), 1)
    meta_ref[...] = jnp.where(lane == 0, jnp.where(pos_ref[0, 0] >= 0, 1, 0), exp_ref[...])


def finish(grad_in, scale_in, master_in, whole_in, grad_ref, scale_ref, master_ref, exp_ref, count_ref, exp_s, count_s, sems):
    copies = [
        pltpu.make_async_copy(src, dst, sems.at[n])
        for n, (src, dst) in enumerate(((grad_in, grad_ref), (scale_in, scale_ref), (master_in, master_ref)))
    ]
    for copy in copies:
        copy.start()
    exp_s[0] = whole_in[0:1, 0:1][0, 0]
    count_s[0] = whole_in[0:1, LANES:LANES + 1][0, 0]
    for n, (src, dst) in enumerate(((exp_s, exp_ref), (count_s, count_ref))):
        copies.append(pltpu.make_async_copy(src, dst, sems.at[3 + n]))
        copies[-1].start()
    for copy in copies:
        copy.wait()


def on_device(partials, scales, overflow_pos, weights, exponent):
    inter_size = lax.axis_size("inter")
    intra_size = lax.axis_size("intra")
    total = inter_size * intra_size
    row_total, full_width = partials.shape[1], partials.shape[2]
    block_total = scales.shape[2]
    block_len = full_width // block_total
    share_cols = full_width // intra_size
    blocks = share_cols // block_len
    width = share_cols // 2 + LANES
    any_space = pl.BlockSpec(memory_space=pl.ANY)
    vmem = pl.BlockSpec(memory_space=pltpu.VMEM)
    smem = pl.BlockSpec(memory_space=pltpu.SMEM)

    def in_vmem(array):
        return pltpu.with_memory_space_constraint(array, pltpu.VMEM)

    meta = pl.pallas_call(
        gather_scalars,
        out_shape=pltpu.VMEM((1, LANES), jnp.int32),
        in_specs=[smem, smem],
        out_specs=vmem,
        cost_estimate=pl.CostEstimate(flops=1000000, bytes_accessed=0, transcendentals=0),
        name="gather_scalars",
    )(overflow_pos, exponent)
    tails = pl.pallas_call(
        functools.partial(prepare, intra_size, width - LANES, block_len),
        out_shape=pltpu.VMEM((row_total, intra_size, 2, LANES), jnp.bfloat16),
        in_specs=[vmem, vmem],
        out_specs=vmem,
        cost_estimate=pl.CostEstimate(flops=PREPARE_FLOPS, bytes_accessed=0, transcendentals=0),
        name="prepare",
    )(in_vmem(meta), in_vmem(scales))
    results = pl.pallas_call(
        functools.partial(exchange, inter_size, intra_size, block_len),
        out_shape=(
            pltpu.VMEM((1, share_cols), jnp.float32),
            pltpu.VMEM((1, blocks), jnp.float32),
            pltpu.VMEM((1, share_cols), jnp.float32),
            pltpu.VMEM((1, 2 * LANES), jnp.int32),
        ),
        in_specs=[vmem, vmem, vmem, any_space],
        out_specs=(vmem, vmem, vmem, vmem),
        scratch_shapes=[
            pltpu.VMEM((1, share_cols), jnp.float32),
            pltpu.VMEM((ROW_GROUP, intra_size, 2, width - LANES), jnp.float32),
            pltpu.VMEM((row_total, intra_size, 2, width), jnp.bfloat16),
            pltpu.VMEM((total, 2, width), jnp.bfloat16),
            pltpu.SemaphoreType.DMA,
            pltpu.SemaphoreType.DMA,
            pltpu.SemaphoreType.DMA,
            pltpu.SemaphoreType.DMA,
            pltpu.SemaphoreType.REGULAR((total // CORES,)),
        ],
        compiler_params=pltpu.CompilerParams(collective_id=0, has_side_effects=True),
        name="exchange",
    )(in_vmem(partials), in_vmem(tails), in_vmem(meta), weights)
    grad_out, block_scale, master_out, new_exponent, count = pl.pallas_call(
        finish,
        out_shape=(
            jax.ShapeDtypeStruct((1, share_cols), jnp.float32),
            jax.ShapeDtypeStruct((1, blocks), jnp.float32),
            jax.ShapeDtypeStruct((1, share_cols), jnp.float32),
            jax.ShapeDtypeStruct((1,), jnp.int32),
            jax.ShapeDtypeStruct((1,), jnp.int32),
        ),
        in_specs=[vmem] * 4,
        out_specs=(any_space,) * 5,
        scratch_shapes=[pltpu.SMEM((1,), jnp.int32), pltpu.SMEM((1,), jnp.int32), pltpu.SemaphoreType.DMA((5,))],
        name="finish",
    )(*(pltpu.with_memory_space_constraint(result, pltpu.VMEM) for result in results))
    return grad_out, block_scale, master_out, new_exponent.reshape(()), count.reshape(())


def solution(mesh):
    placed = (
        P(("inter", "intra"), None, None),
        P(("inter", "intra"), None, None),
        P(("inter", "intra"), None),
        P("inter", "intra"),
        P(),
    )
    return jax.shard_map(
        on_device,
        mesh=mesh,
        in_specs=placed,
        out_specs=(P("inter", "intra"), P("inter", "intra"), P("inter", "intra"), P(), P()),
        check_vma=False,
    )
```

time: 14.2 us -> 13.1 us (0.923)
  Pallas kernels: 12.1 us -> 10.9 us
    pallas_call x1, Pallas kernels: 10.9 us -> 10 us  [on_device(): pl.pallas_call(functools.partial(exchange, inter_size, intra_size, block_...]
    pallas_call x1, Pallas kernels: 1.16 us -> 0.67 us  [on_device(): pl.pallas_call(finish, out_shape=(jax.ShapeDtypeStruct((1, share_cols), j...]
    pallas_call x0 -> x2, Pallas kernels: none -> 0.17 us  [the longest x1 0.17 us: on_device(): pl.pallas_call(functools.partial(prepare, intra_size, width - LANES, bloc...]
where the time goes in v1:
time: 13.1 us; the launch traced here: 12.9 us
  Pallas kernels  10.9 us (83%)
  between operations  2.02 us (15%)
    pallas_call x1, Pallas kernels, on_device(): pl.pallas_call(functools.partial(exchange, inter_size, intra_size, block_...  10 us
    pallas_call x1, Pallas kernels, on_device(): pl.pallas_call(finish, out_shape=(jax.ShapeDtypeStruct((1, share_cols), j...  0.67 us

profile of v1, /device:TPU:0, one launch (start us, length us, event | category | flops | bytes accessed | tf_op | source)
XLA Modules:
  0.0 12.9 jit_solution(5185475532184060598)
XLA Ops:
  0.6 0.0 copy-start.1
  0.6 0.0 copy-start
  2.0 0.0 copy-done.1
  2.0 0.2 %prepare.1.tail_ref = bf16[16,2,2,128]{3,2,1,0:T(2,128)(2,1)S(1)} custom-call(s32[1,128]{1,0:T(1,128)S(1)} %gather_scalars.1.meta_ref, bf16[1,16,20]{2,1,0:T(8,128)(2,1)S(1)} %copy-done.1), custom_call_target="tpu_custom_call" | custom-call | flops 60000000 | tf_op jit(solution)/shard_map/prepare/pallas_call | solution.py:245
  2.2 0.0 copy-done
  2.2 10.0 %exchange.1 = (f32[1,2560]{1,0:T(1,128)S(1)}, f32[1,10]{1,0:T(1,128)S(1)}, f32[1,2560]{1,0:T(1,128)S(1)}, s32[1,256]{1,0:T(1,128)S(1)}) custom-call(bf16[1,16,5120]{2,1,0:T(8,128)(2,1)S(1)} %copy-done, bf16[16,2,2,128]{3,2,1,0:T(2,128)(2,1)S(1)} %prepare.1.tail_ref, s32[1,128]{1,0:T(1,128)S(1)} %gather_scalars.1.meta_ref, f32[1,2560]{1,0:T(1,128)} %w_hbm.1), custom_call_target="tpu_custom_call" | custom-call | tf_op jit(solution)/shard_map/exchange/pallas_call | solution.py:253
  12.2 0.7 %finish.1 = (f32[1,2560]{1,0:T(1,128)}, f32[1,10]{1,0:T(1,128)}, f32[1,2560]{1,0:T(1,128)}, s32[1]{0:T(128)}, s32[1]{0:T(128)}) custom-call(f32[1,2560]{1,0:T(1,128)S(1)} %get-tuple-element.14.grad_in, f32[1,10]{1,0:T(1,128)S(1)} %get-tuple-element.15.scale_in, f32[1,2560]{1,0:T(1,128)S(1)} %get-tuple-element.16.master_in, ...), custom_call_target="tpu_custom_call" | custom-call | tf_op jit(solution)/shard_map/finish/pallas_call | solution.py:277
  (1 shorter events, 0.0 us)
Async XLA Ops:
  0.6 1.4 %copy-start.1 = (bf16[1,16,20]{2,1,0:T(8,128)(2,1)S(1)}, bf16[1,16,20]{2,1,0:T(8,128)(2,1)}, u32[]{:S(2)}) copy-start(bf16[1,16,20]{2,1,0:T(8,128)(2,1)} %s_ref.1) | copy-start | bytes 1924
  0.6 1.5 %copy-start = (bf16[1,16,5120]{2,1,0:T(8,128)(2,1)S(1)}, bf16[1,16,5120]{2,1,0:T(8,128)(2,1)}, u32[]{:S(2)}) copy-start(bf16[1,16,5120]{2,1,0:T(8,128)(2,1)} %x_ref.1) | copy-start | bytes 491524

commit v2 on v1

v2 whole, which is shorter than its diff:
```python
import functools

import jax
import jax.numpy as jnp
from jax import lax
from jax.experimental import pallas as pl
from jax.experimental.pallas import tpu as pltpu
from jax.sharding import PartitionSpec as P

LANES = 128
CORES = 2
LINES = 2
MOST_LAYERS = 8
ROW_GROUP = 16
SOURCE_GROUP = 32
MESH = pl.DeviceIdType.MESH


def exchange(inter_size, intra_size, x_ref, s_ref, meta_ref, w_hbm,
             grad_ref, scale_ref, master_ref, whole_ref,
             w_ref, staged, outgoing, incoming,
             load_sem, own_sem, send_sem, recv_sems, told_sem):
    total = inter_size * intra_size
    row_total, full_width = x_ref.shape[1:]
    block_total = s_ref.shape[2]
    block_len = full_width // block_total
    share_cols = full_width // intra_size
    half = share_cols // 2
    tiles = half // LANES
    layers = inter_size // (CORES * LINES)
    ordered = layers * CORES * LINES == inter_size and layers & (layers - 1) == 0 and layers <= MOST_LAYERS
    my_inter = lax.axis_index("inter")
    my_intra = lax.axis_index("intra")
    me = my_inter * intra_size + my_intra
    my_core = lax.rem(my_inter, CORES)
    place = (my_inter // (CORES * LINES), lax.rem(my_inter // CORES, LINES), my_intra)
    past = tuple(at + 1 for at in place)
    ends = (layers, LINES, intra_size)
    barrier = pltpu.get_barrier_semaphore()

    def each_chip(lows, highs, visit):
        def along_z(z, carry):
            def along_y(y, carry):
                def along_x(x, carry):
                    visit(z, y, x)
                    return carry
                return lax.fori_loop(lows[2], highs[2], along_x, carry)
            return lax.fori_loop(lows[1], highs[1], along_y, carry)
        lax.fori_loop(lows[0], highs[0], along_z, 0)

    def inter_of(z, y, core):
        return (z * LINES + y) * CORES + core

    def signal(semaphore, inter, intra):
        pl.semaphore_signal(semaphore, inc=1, device_id=(inter, intra), device_id_type=MESH)

    def elsewhere(z, y, x):
        return (z != place[0]) | (y != place[1]) | (x != place[2])

    def send(to_inter, to_intra, group):
        pltpu.make_async_remote_copy(
            src_ref=outgoing.at[to_inter, to_intra],
            dst_ref=incoming.at[me],
            send_sem=send_sem,
            recv_sem=recv_sems.at[group],
            device_id=(to_inter, to_intra),
            device_id_type=MESH,
        ).start()

    if ordered:
        def greet(z, y, x):
            @pl.when(elsewhere(z, y, x))
            def _():
                for core in range(CORES):
                    signal(barrier, inter_of(z, y, core), x)

        each_chip(place, ends, greet)

        for core in range(CORES):
            @pl.when(core != my_core)
            def _():
                signal(barrier, inter_of(place[0], place[1], core), my_intra)
    else:
        for n in range(total):
            signal(barrier, n // intra_size, n % intra_size)
    load = pltpu.make_async_copy(w_hbm, w_ref, load_sem)
    load.start()

    flag = meta_ref[0:1, 0:1].astype(jnp.float32)
    shares = 2 * intra_size
    pick_block = lax.broadcasted_iota(jnp.int32, (block_total, shares * LANES), 0)
    pick = lax.broadcasted_iota(jnp.int32, (block_total, shares * LANES), 1)
    pick_lane = pick % LANES
    hit = (pick_block == (pick // LANES * tiles + pick_lane) * LANES // block_len) & (pick_lane < tiles)
    hit = hit.astype(jnp.float32).astype(jnp.bfloat16)
    lane = lax.broadcasted_iota(jnp.int32, (ROW_GROUP, LANES), 1)

    def stage(group, carry):
        rows = pl.ds(pl.multiple_of(group * ROW_GROUP, ROW_GROUP), ROW_GROUP)
        spread = jnp.dot(s_ref[0, rows, :], hit, preferred_element_type=jnp.float32)
        for n in range(shares):
            b, h = divmod(n, 2)
            staged[:, b, h, pl.ds(0, half)] = x_ref[0, rows, pl.ds(n * half, half)].astype(jnp.float32)
            staged[:, b, h, pl.ds(half, LANES)] = jnp.where(lane == tiles, flag, spread[:, n * LANES:(n + 1) * LANES])
        outgoing[rows] = staged[...].astype(jnp.bfloat16)
        return carry

    if row_total == ROW_GROUP:
        stage(0, 0)
    else:
        lax.fori_loop(0, row_total // ROW_GROUP, stage, 0)

    if ordered:
        def send_chip(z, y, x):
            for core in range(CORES):
                @pl.when(elsewhere(z, y, x) | (core != my_core))
                def _():
                    send(inter_of(z, y, core), x, z ^ place[0])

        def send_lower(z, y, x):
            @pl.when(elsewhere(z, y, x) & (z + y + x > 0))
            def _():
                for core in range(CORES):
                    send(inter_of(z, y, core), x, z ^ place[0])

        def tell(z, y, x):
            @pl.when(elsewhere(z, y, x))
            def _():
                steps = place[0] - z + place[1] - y + place[2] - x
                signal(told_sem.at[steps - 1], inter_of(z, y, my_core), x)

        below = past[0] * past[1] * past[2] * CORES - 1
        pl.semaphore_wait(barrier, below)
        @pl.when(place[0] + place[1] + place[2] > 0)
        def _():
            for core in range(CORES):
                send(core, 0, place[0])
        each_chip((0, 0, 0), past, tell)
        each_chip((0, 0, 0), past, send_lower)
        for core in range(CORES):
            @pl.when(core != my_core)
            def _():
                send(inter_of(place[0], place[1], core), my_intra, 0)

        offsets = [(dz, dy, dx) for dz in range(layers) for dy in range(LINES) for dx in range(intra_size)]
        for steps in range(1, sum(ends) - 2):
            level = [offset for offset in offsets if sum(offset) == steps]
            inside = [functools.reduce(jnp.logical_and, [at + d < end for at, d, end in zip(place, offset, ends)])
                      for offset in level]
            uppers = sum(each.astype(jnp.int32) for each in inside)

            @pl.when(uppers > 0)
            def _():
                pl.semaphore_wait(told_sem.at[steps - 1], uppers)

            for offset, each in zip(level, inside):
                @pl.when(each)
                def _():
                    lows = tuple(at + d if d else 0 for at, d in zip(place, offset))
                    highs = tuple(at + d + 1 for at, d in zip(place, offset))
                    each_chip(lows, highs, send_chip)

    else:
        pl.semaphore_wait(barrier, total)
        for n in range(total - 1):
            target = n + (n >= me).astype(jnp.int32)
            send(target // intra_size, lax.rem(target, intra_size), 0)

    own = pltpu.make_async_copy(outgoing.at[my_inter, my_intra], incoming.at[me], own_sem)
    own.start()
    exponent = meta_ref[0:1, 1:2]
    unscale = jnp.exp2(jnp.broadcast_to(-exponent.astype(jnp.float32), (1, LANES)))
    load.wait()
    own.wait()

    def add(first, size, sums):
        sources = pl.ds(first, size)
        factors = incoming[sources, :, pl.ds(half, LANES)].astype(jnp.float32)
        added = [
            jnp.sum(incoming[sources, :, pl.ds(t * LANES, LANES)].astype(jnp.float32) * factors[:, :, t:t + 1], axis=0)
            for t in range(tiles)
        ]
        added.append(jnp.sum(factors, axis=0))
        return tuple(s + a for s, a in zip(sums, added))

    def arrived(group, size):
        landed = incoming.at[pl.ds(0, size)]
        pltpu.make_async_copy(landed, landed, recv_sems.at[group]).wait()

    sums = tuple(jnp.zeros((2, LANES), jnp.float32) for _ in range(tiles + 1))
    if ordered:
        per_layer = total // layers
        for group in range(layers):
            arrived(group, per_layer - (group == 0))
            sums = add((place[0] ^ group) * per_layer, per_layer, sums)
    else:
        arrived(0, total - 1)
        sums = lax.fori_loop(0, total // SOURCE_GROUP, lambda n, sums: add(n * SOURCE_GROUP, SOURCE_GROUP, sums), sums)
    lane = lax.broadcasted_iota(jnp.int32, (1, LANES), 1)
    count = jnp.sum(jnp.where(lane == tiles, sums[tiles][0:1], 0.0), axis=1, keepdims=True).astype(jnp.int32)
    keep = jnp.broadcast_to(count, (1, LANES)) == 0
    per_block = block_len // LANES
    peaks = []
    grads = []
    for t in range(tiles):
        grad = sums[t] * unscale
        grads.append(grad)
        peaks.append(jnp.max(jnp.abs(grad), axis=1, keepdims=True))
    for h in range(2):
        for t in range(tiles):
            grad = grads[t][h:h + 1]
            columns = pl.ds(h * half + t * LANES, LANES)
            grad_ref[0:1, columns] = grad
            weights = w_ref[0:1, columns]
            master_ref[0:1, columns] = jnp.where(keep, weights - 0.5 * grad, weights)
    blocks = share_cols // block_len
    block_lane = lax.broadcasted_iota(jnp.int32, (1, blocks), 1)
    largest = jnp.zeros((1, blocks), jnp.float32)
    for n in range(blocks):
        parts = [divmod(n * per_block + k, tiles) for k in range(per_block)]
        top = functools.reduce(jnp.maximum, [peaks[t][h:h + 1] for h, t in parts])
        largest = jnp.where(block_lane == n, top, largest)
    scale_ref[...] = largest / 127.0
    whole_ref[0:1, pl.ds(0, LANES)] = jnp.broadcast_to(exponent - jnp.where(count > 0, 1, 0), (1, LANES))
    whole_ref[0:1, pl.ds(LANES, LANES)] = jnp.broadcast_to(count, (1, LANES))
    sent = incoming.at[pl.ds(0, total - 1)]
    pltpu.make_async_copy(sent, sent, send_sem).wait()


def gather_scalars(pos_ref, exp_ref, meta_ref):
    lane = lax.broadcasted_iota(jnp.int32, (1, LANES), 1)
    meta_ref[...] = jnp.where(lane == 0, jnp.where(pos_ref[0, 0] >= 0, 1, 0), exp_ref[...])


def pass_scales(meta_ref, s_ref, passed_ref):
    passed_ref[...] = s_ref[...]


def finish(grad_in, scale_in, master_in, whole_in, grad_ref, scale_ref, master_ref, exp_ref, count_ref, exp_s, count_s, sems):
    copies = [
        pltpu.make_async_copy(src, dst, sems.at[n])
        for n, (src, dst) in enumerate(((grad_in, grad_ref), (scale_in, scale_ref), (master_in, master_ref)))
    ]
    for copy in copies:
        copy.start()
    exp_s[0] = whole_in[0:1, 0:1][0, 0]
    count_s[0] = whole_in[0:1, LANES:LANES + 1][0, 0]
    for n, (src, dst) in enumerate(((exp_s, exp_ref), (count_s, count_ref))):
        copies.append(pltpu.make_async_copy(src, dst, sems.at[3 + n]))
        copies[-1].start()
    for copy in copies:
        copy.wait()


def on_device(partials, scales, overflow_pos, weights, exponent):
    inter_size = lax.axis_size("inter")
    intra_size = lax.axis_size("intra")
    total = inter_size * intra_size
    row_total, full_width = partials.shape[1], partials.shape[2]
    block_len = full_width // scales.shape[2]
    share_cols = full_width // intra_size
    blocks = share_cols // block_len
    width = share_cols // 2 + LANES
    layers = inter_size // (CORES * LINES)
    steps = layers + LINES + intra_size - 3
    groups = layers if layers <= MOST_LAYERS else 1
    any_space = pl.BlockSpec(memory_space=pl.ANY)
    vmem = pl.BlockSpec(memory_space=pltpu.VMEM)
    smem = pl.BlockSpec(memory_space=pltpu.SMEM)

    def in_vmem(array):
        return pltpu.with_memory_space_constraint(array, pltpu.VMEM)

    meta = pl.pallas_call(
        gather_scalars,
        out_shape=pltpu.VMEM((1, LANES), jnp.int32),
        in_specs=[smem, smem],
        out_specs=vmem,
        cost_estimate=pl.CostEstimate(flops=1000000, bytes_accessed=0, transcendentals=0),
        name="gather_scalars",
    )(overflow_pos, exponent)
    passed = pl.pallas_call(
        pass_scales,
        out_shape=pltpu.VMEM(scales.shape, scales.dtype),
        in_specs=[vmem, vmem],
        out_specs=vmem,
        cost_estimate=pl.CostEstimate(flops=60000000, bytes_accessed=0, transcendentals=0),
        name="pass_scales",
    )(in_vmem(meta), in_vmem(scales))
    results = pl.pallas_call(
        functools.partial(exchange, inter_size, intra_size),
        out_shape=(
            pltpu.VMEM((1, share_cols), jnp.float32),
            pltpu.VMEM((1, blocks), jnp.float32),
            pltpu.VMEM((1, share_cols), jnp.float32),
            pltpu.VMEM((1, 2 * LANES), jnp.int32),
        ),
        in_specs=[vmem, vmem, vmem, any_space],
        out_specs=(vmem, vmem, vmem, vmem),
        scratch_shapes=[
            pltpu.VMEM((1, share_cols), jnp.float32),
            pltpu.VMEM((ROW_GROUP, intra_size, 2, width), jnp.float32),
            pltpu.VMEM((row_total, intra_size, 2, width), jnp.bfloat16),
            pltpu.VMEM((total, 2, width), jnp.bfloat16),
            pltpu.SemaphoreType.DMA,
            pltpu.SemaphoreType.DMA,
            pltpu.SemaphoreType.DMA,
            pltpu.SemaphoreType.DMA((groups,)),
            pltpu.SemaphoreType.REGULAR((steps,)),
        ],
        compiler_params=pltpu.CompilerParams(collective_id=0, has_side_effects=True),
        name="exchange",
    )(in_vmem(partials), in_vmem(passed), in_vmem(meta), weights)
    grad_out, block_scale, master_out, new_exponent, count = pl.pallas_call(
        finish,
        out_shape=(
            jax.ShapeDtypeStruct((1, share_cols), jnp.float32),
            jax.ShapeDtypeStruct((1, blocks), jnp.float32),
            jax.ShapeDtypeStruct((1, share_cols), jnp.float32),
            jax.ShapeDtypeStruct((1,), jnp.int32),
            jax.ShapeDtypeStruct((1,), jnp.int32),
        ),
        in_specs=[vmem] * 4,
        out_specs=(any_space,) * 5,
        scratch_shapes=[pltpu.SMEM((1,), jnp.int32), pltpu.SMEM((1,), jnp.int32), pltpu.SemaphoreType.DMA((5,))],
        name="finish",
    )(*(in_vmem(result) for result in results))
    return grad_out, block_scale, master_out, new_exponent.reshape(()), count.reshape(())


def solution(mesh):
    placed = (
        P(("inter", "intra"), None, None),
        P(("inter", "intra"), None, None),
        P(("inter", "intra"), None),
        P("inter", "intra"),
        P(),
    )
    return jax.shard_map(
        on_device,
        mesh=mesh,
        in_specs=placed,
        out_specs=(P("inter", "intra"), P("inter", "intra"), P("inter", "intra"), P(), P()),
        check_vma=False,
    )
```

time: 13.1 us -> 12.5 us (0.954)
  Pallas kernels: 10.9 us -> 10.3 us
    pallas_call x2, Pallas kernels: 10.2 us -> 9.66 us  [the longest x1 9.66 us: on_device(): pl.pallas_call(functools.partial(exchange, inter_size, intra_size), out_s...]
where the time goes in v2:
time: 12.5 us; the launch traced here: 12.4 us
  Pallas kernels  10.3 us (82%)
  between operations  2.02 us (16%)
    pallas_call x1, Pallas kernels, on_device(): pl.pallas_call(functools.partial(exchange, inter_size, intra_size), out_s...  9.66 us
    pallas_call x1, Pallas kernels, on_device(): pl.pallas_call(finish, out_shape=(jax.ShapeDtypeStruct((1, share_cols), j...  0.67 us

profile of v2, /device:TPU:0, one launch (start us, length us, event | category | flops | bytes accessed | tf_op | source)
XLA Modules:
  0.0 12.4 jit_solution(7931457247672218208)
XLA Ops:
  0.6 0.0 copy-start.1
  0.6 0.0 copy-start
  2.0 0.0 copy-done.1
  2.0 0.0 copy-done
  2.0 9.7 %exchange.1 = (f32[1,2560]{1,0:T(1,128)S(1)}, f32[1,10]{1,0:T(1,128)S(1)}, f32[1,2560]{1,0:T(1,128)S(1)}, s32[1,256]{1,0:T(1,128)S(1)}) custom-call(bf16[1,16,5120]{2,1,0:T(8,128)(2,1)S(1)} %copy-done, bf16[1,16,20]{2,1,0:T(8,128)(2,1)S(1)} %pass_scales.1.s_ref, s32[1,128]{1,0:T(1,128)S(1)} %gather_scalars.1.meta_ref, f32[1,2560]{1,0:T(1,128)} %w_hbm.1), custom_call_target="tpu_custom_call" | custom-call | tf_op jit(solution)/shard_map/exchange/pallas_call | solution.py:290
  11.7 0.7 %finish.1 = (f32[1,2560]{1,0:T(1,128)}, f32[1,10]{1,0:T(1,128)}, f32[1,2560]{1,0:T(1,128)}, s32[1]{0:T(128)}, s32[1]{0:T(128)}) custom-call(f32[1,2560]{1,0:T(1,128)S(1)} %get-tuple-element.14.grad_in, f32[1,10]{1,0:T(1,128)S(1)} %get-tuple-element.15.scale_in, f32[1,2560]{1,0:T(1,128)S(1)} %get-tuple-element.16.master_in, ...), custom_call_target="tpu_custom_call" | custom-call | tf_op jit(solution)/shard_map/finish/pallas_call | solution.py:314
  (2 shorter events, 0.0 us)
Async XLA Ops:
  0.6 1.4 %copy-start.1 = (bf16[1,16,20]{2,1,0:T(8,128)(2,1)S(1)}, bf16[1,16,20]{2,1,0:T(8,128)(2,1)}, u32[]{:S(2)}) copy-start(bf16[1,16,20]{2,1,0:T(8,128)(2,1)} %s_ref.1) | copy-start | bytes 1924
  0.6 1.4 %copy-start = (bf16[1,16,5120]{2,1,0:T(8,128)(2,1)S(1)}, bf16[1,16,5120]{2,1,0:T(8,128)(2,1)}, u32[]{:S(2)}) copy-start(bf16[1,16,5120]{2,1,0:T(8,128)(2,1)} %x_ref.1) | copy-start | bytes 491524

commit v3 on v2

--- a/solution.py
+++ b/solution.py
@@ -11,29 +11,37 @@
 CORES = 2
 LINES = 2
 MOST_LAYERS = 8
-ROW_GROUP = 16
+KEEPER = CORES - 1
+TAIL = 128
+ROW_GROUP = 8
 SOURCE_GROUP = 32
 MESH = pl.DeviceIdType.MESH
 
 
-def exchange(inter_size, intra_size, x_ref, s_ref, meta_ref, w_hbm,
+def layers_of(inter_size):
+    layers = inter_size // (CORES * LINES)
+    return layers, layers * CORES * LINES == inter_size and 1 < layers <= MOST_LAYERS
+
+
+def exchange(inter_size, intra_size, block_len, x_ref, s_ref, meta_ref, w_hbm,
              grad_ref, scale_ref, master_ref, whole_ref,
-             w_ref, staged, outgoing, incoming,
-             load_sem, own_sem, send_sem, recv_sems, told_sem):
+             w_ref, staged, outgoing, incoming, layer_in, layer_sum, sum_in,
+             load_sem, own_sem, send_sem, sum_send_sem, recv_sems, layer_sems, told_sem, mate_sem):
     total = inter_size * intra_size
     row_total, full_width = x_ref.shape[1:]
-    block_total = s_ref.shape[2]
-    block_len = full_width // block_total
     share_cols = full_width // intra_size
     half = share_cols // 2
     tiles = half // LANES
-    layers = inter_size // (CORES * LINES)
-    ordered = layers * CORES * LINES == inter_size and layers & (layers - 1) == 0 and layers <= MOST_LAYERS
+    layers, ordered = layers_of(inter_size)
+    per_layer = total // layers if ordered else total
+    scale_tiles = block_len // LANES if half % block_len == 0 else 1
+    scale_lanes = tiles // scale_tiles
     my_inter = lax.axis_index("inter")
     my_intra = lax.axis_index("intra")
     me = my_inter * intra_size + my_intra
     my_core = lax.rem(my_inter, CORES)
     place = (my_inter // (CORES * LINES), lax.rem(my_inter // CORES, LINES), my_intra)
+    at_first = place[0] + place[1] + place[2] == 0
     past = tuple(at + 1 for at in place)
     ends = (layers, LINES, intra_size)
     barrier = pltpu.get_barrier_semaphore()
@@ -71,15 +79,15 @@
         def greet(z, y, x):
             @pl.when(elsewhere(z, y, x))
             def _():
-                for core in range(CORES):
-                    signal(barrier, inter_of(z, y, core), x)
+                signal(barrier, inter_of(z, y, KEEPER), x)
+                for core in range(KEEPER):
+                    pl.when(at_first)(functools.partial(signal, barrier, inter_of(z, y, core), x))
 
         each_chip(place, ends, greet)
-
-        for core in range(CORES):
-            @pl.when(core != my_core)
-            def _():
-                signal(barrier, inter_of(place[0], place[1], core), my_intra)
+        pl.when(my_core != KEEPER)(lambda: signal(barrier, inter_of(place[0], place[1], KEEPER), my_intra))
+        for core in range(KEEPER):
+            pl.when(at_first & (my_core == KEEPER))(
+                functools.partial(signal, barrier, inter_of(place[0], place[1], core), my_intra))
     else:
         for n in range(total):
             signal(barrier, n // intra_size, n % intra_size)
@@ -88,63 +96,97 @@
 
     flag = meta_ref[0:1, 0:1].astype(jnp.float32)
     shares = 2 * intra_size
-    pick_block = lax.broadcasted_iota(jnp.int32, (block_total, shares * LANES), 0)
-    pick = lax.broadcasted_iota(jnp.int32, (block_total, shares * LANES), 1)
-    pick_lane = pick % LANES
-    hit = (pick_block == (pick // LANES * tiles + pick_lane) * LANES // block_len) & (pick_lane < tiles)
-    hit = hit.astype(jnp.float32).astype(jnp.bfloat16)
-    lane = lax.broadcasted_iota(jnp.int32, (ROW_GROUP, LANES), 1)
+    lane = lax.broadcasted_iota(jnp.int32, (ROW_GROUP, TAIL), 1)
+    flags = jnp.where(lane == scale_lanes, flag, 0.0)
 
     def stage(group, carry):
         rows = pl.ds(pl.multiple_of(group * ROW_GROUP, ROW_GROUP), ROW_GROUP)
-        spread = jnp.dot(s_ref[0, rows, :], hit, preferred_element_type=jnp.float32)
+        scale_rows = s_ref[0, rows, :]
         for n in range(shares):
             b, h = divmod(n, 2)
+            if scale_tiles > 1:
+                spread = pltpu.roll(scale_rows, (LANES - n * scale_lanes) % LANES, 1)[:, :TAIL]
+                spread = jnp.where(lane < scale_lanes, spread, flags)
+            else:
+                spread = flags
+                for t in range(tiles):
+                    block = (n * tiles + t) * LANES // block_len
+                    spread = jnp.where(lane == t, scale_rows[:, block:block + 1], spread)
             staged[:, b, h, pl.ds(0, half)] = x_ref[0, rows, pl.ds(n * half, half)].astype(jnp.float32)
-            staged[:, b, h, pl.ds(half, LANES)] = jnp.where(lane == tiles, flag, spread[:, n * LANES:(n + 1) * LANES])
+            staged[:, b, h, pl.ds(half, TAIL)] = spread
         outgoing[rows] = staged[...].astype(jnp.bfloat16)
         return carry
 
-    if row_total == ROW_GROUP:
-        stage(0, 0)
-    else:
-        lax.fori_loop(0, row_total // ROW_GROUP, stage, 0)
+    stage(0, 0)
+
+    def stage_rest():
+        if row_total == 2 * ROW_GROUP:
+            stage(1, 0)
+        else:
+            lax.fori_loop(1, row_total // ROW_GROUP, stage, 0)
 
     if ordered:
+        flat = LINES + intra_size - 2
+        my_slot = lax.rem(me, per_layer)
+
         def send_chip(z, y, x):
             for core in range(CORES):
-                @pl.when(elsewhere(z, y, x) | (core != my_core))
+                send(inter_of(z, y, core), x, place[0] - z)
+
+        def send_other(z, y, x):
+            pl.when(elsewhere(z, y, x) & (z + y + x > 0))(lambda: send_chip(z, y, x))
+
+        def send_above(z, y, x, core):
+            for up in range(1, layers):
+                @pl.when(z + up < layers)
                 def _():
-                    send(inter_of(z, y, core), x, z ^ place[0])
-
-        def send_lower(z, y, x):
-            @pl.when(elsewhere(z, y, x) & (z + y + x > 0))
+                    pltpu.make_async_remote_copy(
+                        src_ref=outgoing.at[inter_of(z + up, y, core), x],
+                        dst_ref=layer_in.at[up - 1, my_slot],
+                        send_sem=send_sem,
+                        recv_sem=layer_sems.at[up - 1],
+                        device_id=(inter_of(z, y, core), x),
+                        device_id_type=MESH,
+                    ).start()
+
+        def send_chip_above(z, y, x):
+            @pl.when(elsewhere(z, y, x))
             def _():
                 for core in range(CORES):
-                    send(inter_of(z, y, core), x, z ^ place[0])
-
-        def tell(z, y, x):
+                    send_above(z, y, x, core)
+
+        def tell_flat(z, y, x):
             @pl.when(elsewhere(z, y, x))
             def _():
-                steps = place[0] - z + place[1] - y + place[2] - x
-                signal(told_sem.at[steps - 1], inter_of(z, y, my_core), x)
-
-        below = past[0] * past[1] * past[2] * CORES - 1
-        pl.semaphore_wait(barrier, below)
-        @pl.when(place[0] + place[1] + place[2] > 0)
-        def _():
-            for core in range(CORES):
-                send(core, 0, place[0])
-        each_chip((0, 0, 0), past, tell)
-        each_chip((0, 0, 0), past, send_lower)
+                signal(told_sem.at[place[1] - y + place[2] - x - 1], inter_of(z, y, my_core), x)
+
+        def tell_down(z, y, x):
+            @pl.when(elsewhere(z, y, x))
+            def _():
+                signal(told_sem.at[flat + place[0] - z - 1], inter_of(z, y, my_core), x)
+
+        keeps = my_core == KEEPER
+        below = past[0] * past[1] * past[2] * CORES - CORES
+        pl.when(keeps)(stage_rest)
+        pl.semaphore_wait(barrier, jnp.where(keeps, below + KEEPER, jnp.where(at_first, 1, CORES)))
+        pl.when(~at_first)(lambda: send_chip(0, 0, 0))
+        pl.when(~keeps)(stage_rest)
+        for core in range(KEEPER):
+            pl.when(keeps)(functools.partial(signal, mate_sem, inter_of(place[0], place[1], core), my_intra))
+        pl.when(~keeps)(lambda: pl.semaphore_wait(mate_sem, 1))
+        each_chip((place[0], 0, 0), past, tell_flat)
+        each_chip((0, place[1], place[2]), past, tell_down)
+        each_chip((0, 0, 0), past, send_other)
+        each_chip((place[0], 0, 0), past, send_chip_above)
         for core in range(CORES):
             @pl.when(core != my_core)
             def _():
                 send(inter_of(place[0], place[1], core), my_intra, 0)
-
-        offsets = [(dz, dy, dx) for dz in range(layers) for dy in range(LINES) for dx in range(intra_size)]
-        for steps in range(1, sum(ends) - 2):
-            level = [offset for offset in offsets if sum(offset) == steps]
+                send_above(*place, core)
+
+        offsets = [(dy, dx) for dy in range(LINES) for dx in range(intra_size)]
+        for steps in range(1, flat + 1):
+            level = [(0, *offset) for offset in offsets if sum(offset) == steps]
             inside = [functools.reduce(jnp.logical_and, [at + d < end for at, d, end in zip(place, offset, ends)])
                       for offset in level]
             uppers = sum(each.astype(jnp.int32) for each in inside)
@@ -158,9 +200,10 @@
                 def _():
                     lows = tuple(at + d if d else 0 for at, d in zip(place, offset))
                     highs = tuple(at + d + 1 for at, d in zip(place, offset))
+                    each_chip((place[0], *lows[1:]), highs, send_chip_above)
                     each_chip(lows, highs, send_chip)
-
     else:
+        stage_rest()
         pl.semaphore_wait(barrier, total)
         for n in range(total - 1):
             target = n + (n >= me).astype(jnp.int32)
@@ -173,31 +216,61 @@
     load.wait()
     own.wait()
 
-    def add(first, size, sums):
-        sources = pl.ds(first, size)
-        factors = incoming[sources, :, pl.ds(half, LANES)].astype(jnp.float32)
+    def add(ref, sources, sums):
+        factors = ref[sources, :, pl.ds(half, TAIL)].astype(jnp.float32)
+        spread = [jnp.broadcast_to(factors[:, :, n:n + 1], (*factors.shape[:2], LANES)) for n in range(scale_lanes)]
         added = [
-            jnp.sum(incoming[sources, :, pl.ds(t * LANES, LANES)].astype(jnp.float32) * factors[:, :, t:t + 1], axis=0)
+            jnp.sum(ref[sources, :, pl.ds(t * LANES, LANES)].astype(jnp.float32) * spread[t // scale_tiles], axis=0)
             for t in range(tiles)
         ]
         added.append(jnp.sum(factors, axis=0))
         return tuple(s + a for s, a in zip(sums, added))
 
-    def arrived(group, size):
-        landed = incoming.at[pl.ds(0, size)]
-        pltpu.make_async_copy(landed, landed, recv_sems.at[group]).wait()
-
-    sums = tuple(jnp.zeros((2, LANES), jnp.float32) for _ in range(tiles + 1))
+    def landed(ref, semaphore):
+        pltpu.make_async_copy(ref, ref, semaphore).wait()
+
+    sums = tuple(jnp.zeros((2, LANES), jnp.float32) for _ in range(tiles)) + (jnp.zeros((2, TAIL), jnp.float32),)
+    none = sums
     if ordered:
-        per_layer = total // layers
-        for group in range(layers):
-            arrived(group, per_layer - (group == 0))
-            sums = add((place[0] ^ group) * per_layer, per_layer, sums)
+        for up in reversed(range(1, layers)):
+            @pl.when(place[0] + up < layers)
+            def _():
+                mine = pltpu.make_async_copy(
+                    outgoing.at[inter_of(place[0] + up, place[1], my_core), my_intra], layer_in.at[up - 1, my_slot], own_sem)
+                mine.start()
+                mine.wait()
+                landed(layer_in.at[up - 1, pl.ds(0, per_layer - 1)], layer_sems.at[up - 1])
+                for t, each in enumerate(add(layer_in.at[up - 1], pl.ds(0, per_layer), none)):
+                    layer_sum[up - 1, :, pl.ds(t * LANES, each.shape[1])] = each
+                pl.semaphore_wait(told_sem.at[flat + up - 1], 1)
+                pltpu.make_async_remote_copy(
+                    src_ref=layer_sum.at[up - 1],
+                    dst_ref=sum_in.at[up - 1],
+                    send_sem=sum_send_sem,
+                    recv_sem=recv_sems.at[layers - up],
+                    device_id=(inter_of(place[0] + up, place[1], my_core), my_intra),
+                    device_id_type=MESH,
+                ).start()
+
+        landed(incoming.at[pl.ds(0, per_layer - 1)], recv_sems.at[0])
+        sums = add(incoming, pl.ds(place[0] * per_layer, per_layer), sums)
+        for group in range(1, layers):
+            def direct(sums, group=group):
+                landed(incoming.at[pl.ds(0, per_layer)], recv_sems.at[group])
+                return add(incoming, pl.ds((place[0] + group) * per_layer, per_layer), sums)
+
+            def summed(sums, group=group):
+                below = sum_in.at[layers - group - 1]
+                landed(below, recv_sems.at[group])
+                return tuple(each + below[:, pl.ds(t * LANES, each.shape[1])] for t, each in enumerate(sums))
+
+            sums = lax.cond(place[0] + group < layers, direct, summed, sums)
     else:
-        arrived(0, total - 1)
-        sums = lax.fori_loop(0, total // SOURCE_GROUP, lambda n, sums: add(n * SOURCE_GROUP, SOURCE_GROUP, sums), sums)
-    lane = lax.broadcasted_iota(jnp.int32, (1, LANES), 1)
-    count = jnp.sum(jnp.where(lane == tiles, sums[tiles][0:1], 0.0), axis=1, keepdims=True).astype(jnp.int32)
+        landed(incoming.at[pl.ds(0, total - 1)], recv_sems.at[0])
+        sums = lax.fori_loop(
+            0, total // SOURCE_GROUP, lambda n, sums: add(incoming, pl.ds(n * SOURCE_GROUP, SOURCE_GROUP), sums), sums)
+    lane = lax.broadcasted_iota(jnp.int32, (1, TAIL), 1)
+    count = jnp.sum(jnp.where(lane == scale_lanes, sums[tiles][0:1], 0.0), axis=1, keepdims=True).astype(jnp.int32)
     keep = jnp.broadcast_to(count, (1, LANES)) == 0
     per_block = block_len // LANES
     peaks = []
@@ -223,8 +296,17 @@
     scale_ref[...] = largest / 127.0
     whole_ref[0:1, pl.ds(0, LANES)] = jnp.broadcast_to(exponent - jnp.where(count > 0, 1, 0), (1, LANES))
     whole_ref[0:1, pl.ds(LANES, LANES)] = jnp.broadcast_to(count, (1, LANES))
-    sent = incoming.at[pl.ds(0, total - 1)]
-    pltpu.make_async_copy(sent, sent, send_sem).wait()
+    def sent(layer):
+        above = layers - 1 - layer
+        landed(incoming.at[pl.ds(0, per_layer * (layer + 1) - 1 + (per_layer - 1) * above)], send_sem)
+        if above:
+            landed(layer_sum.at[pl.ds(0, above)], sum_send_sem)
+
+    if ordered:
+        for layer in range(layers):
+            pl.when(place[0] == layer)(functools.partial(sent, layer))
+    else:
+        landed(incoming.at[pl.ds(0, total - 1)], send_sem)
 
 
 def gather_scalars(pos_ref, exp_ref, meta_ref):
@@ -233,7 +315,7 @@
 
 
 def pass_scales(meta_ref, s_ref, passed_ref):
-    passed_ref[...] = s_ref[...]
+    passed_ref[0, :, pl.ds(0, s_ref.shape[2])] = s_ref[0].astype(jnp.float32)
 
 
 def finish(grad_in, scale_in, master_in, whole_in, grad_ref, scale_ref, master_ref, exp_ref, count_ref, exp_s, count_s, sems):
@@ -260,10 +342,9 @@
     block_len = full_width // scales.shape[2]
     share_cols = full_width // intra_size
     blocks = share_cols // block_len
-    width = share_cols // 2 + LANES
-    layers = inter_size // (CORES * LINES)
-    steps = layers + LINES + intra_size - 3
-    groups = layers if layers <= MOST_LAYERS else 1
+    width = share_cols // 2 + TAIL
+    layers, ordered = layers_of(inter_size)
+    groups, aboves, per_layer = (layers, layers - 1, total // layers) if ordered else (1, 1, 1)
     any_space = pl.BlockSpec(memory_space=pl.ANY)
     vmem = pl.BlockSpec(memory_space=pltpu.VMEM)
     smem = pl.BlockSpec(memory_space=pltpu.SMEM)
@@ -281,14 +362,14 @@
     )(overflow_pos, exponent)
     passed = pl.pallas_call(
         pass_scales,
-        out_shape=pltpu.VMEM(scales.shape, scales.dtype),
+        out_shape=pltpu.VMEM((1, row_total, LANES), jnp.float32),
         in_specs=[vmem, vmem],
         out_specs=vmem,
         cost_estimate=pl.CostEstimate(flops=60000000, bytes_accessed=0, transcendentals=0),
         name="pass_scales",
     )(in_vmem(meta), in_vmem(scales))
     results = pl.pallas_call(
-        functools.partial(exchange, inter_size, intra_size),
+        functools.partial(exchange, inter_size, intra_size, block_len),
         out_shape=(
             pltpu.VMEM((1, share_cols), jnp.float32),
             pltpu.VMEM((1, blocks), jnp.float32),
@@ -302,11 +383,17 @@
             pltpu.VMEM((ROW_GROUP, intra_size, 2, width), jnp.float32),
             pltpu.VMEM((row_total, intra_size, 2, width), jnp.bfloat16),
             pltpu.VMEM((total, 2, width), jnp.bfloat16),
+            pltpu.VMEM((aboves, per_layer, 2, width), jnp.bfloat16),
+            pltpu.VMEM((aboves, 2, width), jnp.float32),
+            pltpu.VMEM((aboves, 2, width), jnp.float32),
+            pltpu.SemaphoreType.DMA,
             pltpu.SemaphoreType.DMA,
             pltpu.SemaphoreType.DMA,
             pltpu.SemaphoreType.DMA,
             pltpu.SemaphoreType.DMA((groups,)),
-            pltpu.SemaphoreType.REGULAR((steps,)),
+            pltpu.SemaphoreType.DMA((aboves,)),
+            pltpu.SemaphoreType.REGULAR((LINES + intra_size - 2 + aboves,)),
+            pltpu.SemaphoreType.REGULAR,
         ],
         compiler_params=pltpu.CompilerParams(collective_id=0, has_side_effects=True),
         name="exchange",

time: 12.5 us -> 12.2 us (0.976)
  Pallas kernels: 10.3 us -> 10 us
    pallas_call x2, Pallas kernels: 9.66 us -> 9.37 us  [the longest x1 9.36 us: on_device(): pl.pallas_call(functools.partial(exchange, inter_size, intra_size, block_...]
where the time goes in v3:
time: 12.2 us; the launch traced here: 12.1 us
  Pallas kernels  10 us (82%)
  between operations  2.01 us (16%)
    pallas_call x1, Pallas kernels, on_device(): pl.pallas_call(functools.partial(exchange, inter_size, intra_size, block_...  9.36 us
    pallas_call x1, Pallas kernels, on_device(): pl.pallas_call(finish, out_shape=(jax.ShapeDtypeStruct((1, share_cols), j...  0.67 us

profile of v3, /device:TPU:0, one launch (start us, length us, event | category | flops | bytes accessed | tf_op | source)
XLA Modules:
  0.0 12.1 jit_solution(16893494919456442795)
XLA Ops:
  0.6 0.0 copy-start.1
  0.6 0.0 copy-start
  2.0 0.0 copy-done.1
  2.0 0.0 copy-done
  2.0 9.4 %exchange.1 = (f32[1,2560]{1,0:T(1,128)S(1)}, f32[1,10]{1,0:T(1,128)S(1)}, f32[1,2560]{1,0:T(1,128)S(1)}, s32[1,256]{1,0:T(1,128)S(1)}) custom-call(bf16[1,16,5120]{2,1,0:T(8,128)(2,1)S(1)} %copy-done, f32[1,16,128]{2,1,0:T(8,128)S(1)} %pass_scales.1.s_ref, s32[1,128]{1,0:T(1,128)S(1)} %gather_scalars.1.meta_ref, f32[1,2560]{1,0:T(1,128)} %w_hbm.1), custom_call_target="tpu_custom_call" | custom-call | tf_op jit(solution)/shard_map/exchange/pallas_call | solution.py:371
  11.4 0.7 %finish.1 = (f32[1,2560]{1,0:T(1,128)}, f32[1,10]{1,0:T(1,128)}, f32[1,2560]{1,0:T(1,128)}, s32[1]{0:T(128)}, s32[1]{0:T(128)}) custom-call(f32[1,2560]{1,0:T(1,128)S(1)} %get-tuple-element.14.grad_in, f32[1,10]{1,0:T(1,128)S(1)} %get-tuple-element.15.scale_in, f32[1,2560]{1,0:T(1,128)S(1)} %get-tuple-element.16.master_in, ...), custom_call_target="tpu_custom_call" | custom-call | tf_op jit(solution)/shard_map/finish/pallas_call | solution.py:401
  (2 shorter events, 0.0 us)
Async XLA Ops:
  0.6 1.4 %copy-start.1 = (bf16[1,16,20]{2,1,0:T(8,128)(2,1)S(1)}, bf16[1,16,20]{2,1,0:T(8,128)(2,1)}, u32[]{:S(2)}) copy-start(bf16[1,16,20]{2,1,0:T(8,128)(2,1)} %s_ref.1) | copy-start | bytes 1924
  0.6 1.4 %copy-start = (bf16[1,16,5120]{2,1,0:T(8,128)(2,1)S(1)}, bf16[1,16,5120]{2,1,0:T(8,128)(2,1)}, u32[]{:S(2)}) copy-start(bf16[1,16,5120]{2,1,0:T(8,128)(2,1)} %x_ref.1) | copy-start | bytes 491524

commit v4 on v3

--- a/solution.py
+++ b/solution.py
@@ -24,9 +24,9 @@
 
 
 def exchange(inter_size, intra_size, block_len, x_ref, s_ref, meta_ref, w_hbm,
-             grad_ref, scale_ref, master_ref, whole_ref,
+             grad_ref, scale_ref, master_ref, exp_ref, count_ref,
              w_ref, staged, outgoing, incoming, layer_in, layer_sum, sum_in,
-             load_sem, own_sem, send_sem, sum_send_sem, recv_sems, layer_sems, told_sem, mate_sem):
+             load_sem, send_sem, sum_send_sem, recv_sems, layer_sem, told_sem, mate_sem):
     total = inter_size * intra_size
     row_total, full_width = x_ref.shape[1:]
     share_cols = full_width // intra_size
@@ -95,46 +95,52 @@
     load.start()
 
     flag = meta_ref[0:1, 0:1].astype(jnp.float32)
-    shares = 2 * intra_size
     lane = lax.broadcasted_iota(jnp.int32, (ROW_GROUP, TAIL), 1)
     flags = jnp.where(lane == scale_lanes, flag, 0.0)
 
-    def stage(group, carry):
+    def stage(group, shares):
         rows = pl.ds(pl.multiple_of(group * ROW_GROUP, ROW_GROUP), ROW_GROUP)
         scale_rows = s_ref[0, rows, :]
-        for n in range(shares):
-            b, h = divmod(n, 2)
-            if scale_tiles > 1:
-                spread = pltpu.roll(scale_rows, (LANES - n * scale_lanes) % LANES, 1)[:, :TAIL]
-                spread = jnp.where(lane < scale_lanes, spread, flags)
-            else:
-                spread = flags
-                for t in range(tiles):
-                    block = (n * tiles + t) * LANES // block_len
-                    spread = jnp.where(lane == t, scale_rows[:, block:block + 1], spread)
-            staged[:, b, h, pl.ds(0, half)] = x_ref[0, rows, pl.ds(n * half, half)].astype(jnp.float32)
-            staged[:, b, h, pl.ds(half, TAIL)] = spread
-        outgoing[rows] = staged[...].astype(jnp.bfloat16)
-        return carry
-
-    stage(0, 0)
+        for b in shares:
+            for h in range(2):
+                n = b * 2 + h
+                if scale_tiles > 1:
+                    spread = pltpu.roll(scale_rows, (LANES - n * scale_lanes) % LANES, 1)[:, :TAIL]
+                    spread = jnp.where(lane < scale_lanes, spread, flags)
+                else:
+                    spread = flags
+                    for t in range(tiles):
+                        block = (n * tiles + t) * LANES // block_len
+                        spread = jnp.where(lane == t, scale_rows[:, block:block + 1], spread)
+                staged[:, b, h, pl.ds(0, half)] = x_ref[0, rows, pl.ds(n * half, half)].astype(jnp.float32)
+                staged[:, b, h, pl.ds(half, TAIL)] = spread
+            outgoing[rows, b] = staged[:, b].astype(jnp.bfloat16)
+
+    stage(0, range(1))
 
     def stage_rest():
+        stage(0, range(1, intra_size))
         if row_total == 2 * ROW_GROUP:
-            stage(1, 0)
+            stage(1, range(intra_size))
         else:
-            lax.fori_loop(1, row_total // ROW_GROUP, stage, 0)
+            lax.fori_loop(1, row_total // ROW_GROUP, lambda n, carry: (stage(n, range(intra_size)), carry)[1], 0)
 
     if ordered:
         flat = LINES + intra_size - 2
         my_slot = lax.rem(me, per_layer)
 
-        def send_chip(z, y, x):
-            for core in range(CORES):
+        def send_chip(z, y, x, cores=tuple(reversed(range(CORES)))):
+            for core in cores:
                 send(inter_of(z, y, core), x, place[0] - z)
 
-        def send_other(z, y, x):
-            pl.when(elsewhere(z, y, x) & (z + y + x > 0))(lambda: send_chip(z, y, x))
+        def send_planes(lows, highs, keep):
+            def along(z, carry):
+                for core in reversed(range(CORES)):
+                    def visit(z, y, x):
+                        pl.when(keep(z, y, x))(lambda: send_chip(z, y, x, (core,)))
+                    each_chip((z, *lows[1:]), (z + 1, *highs[1:]), visit)
+                return carry
+            lax.fori_loop(lows[0], highs[0], along, 0)
 
         def send_above(z, y, x, core):
             for up in range(1, layers):
@@ -144,7 +150,7 @@
                         src_ref=outgoing.at[inter_of(z + up, y, core), x],
                         dst_ref=layer_in.at[up - 1, my_slot],
                         send_sem=send_sem,
-                        recv_sem=layer_sems.at[up - 1],
+                        recv_sem=layer_sem,
                         device_id=(inter_of(z, y, core), x),
                         device_id_type=MESH,
                     ).start()
@@ -163,20 +169,20 @@
         def tell_down(z, y, x):
             @pl.when(elsewhere(z, y, x))
             def _():
-                signal(told_sem.at[flat + place[0] - z - 1], inter_of(z, y, my_core), x)
+                signal(told_sem.at[flat], inter_of(z, y, my_core), x)
 
         keeps = my_core == KEEPER
         below = past[0] * past[1] * past[2] * CORES - CORES
         pl.when(keeps)(stage_rest)
         pl.semaphore_wait(barrier, jnp.where(keeps, below + KEEPER, jnp.where(at_first, 1, CORES)))
-        pl.when(~at_first)(lambda: send_chip(0, 0, 0))
+        pl.when(~at_first)(lambda: send_chip(0, 0, 0, tuple(range(CORES))))
         pl.when(~keeps)(stage_rest)
         for core in range(KEEPER):
             pl.when(keeps)(functools.partial(signal, mate_sem, inter_of(place[0], place[1], core), my_intra))
         pl.when(~keeps)(lambda: pl.semaphore_wait(mate_sem, 1))
         each_chip((place[0], 0, 0), past, tell_flat)
         each_chip((0, place[1], place[2]), past, tell_down)
-        each_chip((0, 0, 0), past, send_other)
+        send_planes((0, 0, 0), past, lambda z, y, x: elsewhere(z, y, x) & (z + y + x > 0))
         each_chip((place[0], 0, 0), past, send_chip_above)
         for core in range(CORES):
             @pl.when(core != my_core)
@@ -201,7 +207,7 @@
                     lows = tuple(at + d if d else 0 for at, d in zip(place, offset))
                     highs = tuple(at + d + 1 for at, d in zip(place, offset))
                     each_chip((place[0], *lows[1:]), highs, send_chip_above)
-                    each_chip(lows, highs, send_chip)
+                    send_planes(lows, highs, lambda z, y, x: True)
     else:
         stage_rest()
         pl.semaphore_wait(barrier, total)
@@ -209,12 +215,10 @@
             target = n + (n >= me).astype(jnp.int32)
             send(target // intra_size, lax.rem(target, intra_size), 0)
 
-    own = pltpu.make_async_copy(outgoing.at[my_inter, my_intra], incoming.at[me], own_sem)
-    own.start()
+    incoming[me] = outgoing[my_inter, my_intra]
     exponent = meta_ref[0:1, 1:2]
     unscale = jnp.exp2(jnp.broadcast_to(-exponent.astype(jnp.float32), (1, LANES)))
     load.wait()
-    own.wait()
 
     def add(ref, sources, sums):
         factors = ref[sources, :, pl.ds(half, TAIL)].astype(jnp.float32)
@@ -232,17 +236,19 @@
     sums = tuple(jnp.zeros((2, LANES), jnp.float32) for _ in range(tiles)) + (jnp.zeros((2, TAIL), jnp.float32),)
     none = sums
     if ordered:
+        for layer in range(layers - 1):
+            @pl.when(place[0] == layer)
+            def _():
+                above = layers - 1 - layer
+                landed(layer_in.at[pl.ds(0, above), pl.ds(0, per_layer - 1)], layer_sem)
+                pl.semaphore_wait(told_sem.at[flat], above)
+
         for up in reversed(range(1, layers)):
             @pl.when(place[0] + up < layers)
             def _():
-                mine = pltpu.make_async_copy(
-                    outgoing.at[inter_of(place[0] + up, place[1], my_core), my_intra], layer_in.at[up - 1, my_slot], own_sem)
-                mine.start()
-                mine.wait()
-                landed(layer_in.at[up - 1, pl.ds(0, per_layer - 1)], layer_sems.at[up - 1])
+                layer_in[up - 1, my_slot] = outgoing[inter_of(place[0] + up, place[1], my_core), my_intra]
                 for t, each in enumerate(add(layer_in.at[up - 1], pl.ds(0, per_layer), none)):
                     layer_sum[up - 1, :, pl.ds(t * LANES, each.shape[1])] = each
-                pl.semaphore_wait(told_sem.at[flat + up - 1], 1)
                 pltpu.make_async_remote_copy(
                     src_ref=layer_sum.at[up - 1],
                     dst_ref=sum_in.at[up - 1],
@@ -294,8 +300,10 @@
         top = functools.reduce(jnp.maximum, [peaks[t][h:h + 1] for h, t in parts])
         largest = jnp.where(block_lane == n, top, largest)
     scale_ref[...] = largest / 127.0
-    whole_ref[0:1, pl.ds(0, LANES)] = jnp.broadcast_to(exponent - jnp.where(count > 0, 1, 0), (1, LANES))
-    whole_ref[0:1, pl.ds(LANES, LANES)] = jnp.broadcast_to(count, (1, LANES))
+    total_count = count[0, 0]
+    exp_ref[0] = exponent[0, 0] - jnp.where(total_count > 0, 1, 0)
+    count_ref[0] = total_count
+
     def sent(layer):
         above = layers - 1 - layer
         landed(incoming.at[pl.ds(0, per_layer * (layer + 1) - 1 + (per_layer - 1) * above)], send_sem)
@@ -318,18 +326,11 @@
     passed_ref[0, :, pl.ds(0, s_ref.shape[2])] = s_ref[0].astype(jnp.float32)
 
 
-def finish(grad_in, scale_in, master_in, whole_in, grad_ref, scale_ref, master_ref, exp_ref, count_ref, exp_s, count_s, sems):
-    copies = [
-        pltpu.make_async_copy(src, dst, sems.at[n])
-        for n, (src, dst) in enumerate(((grad_in, grad_ref), (scale_in, scale_ref), (master_in, master_ref)))
-    ]
+def finish(*refs):
+    half = (len(refs) - 1) // 2
+    copies = [pltpu.make_async_copy(src, dst, refs[-1].at[n]) for n, (src, dst) in enumerate(zip(refs[:half], refs[half:-1]))]
     for copy in copies:
         copy.start()
-    exp_s[0] = whole_in[0:1, 0:1][0, 0]
-    count_s[0] = whole_in[0:1, LANES:LANES + 1][0, 0]
-    for n, (src, dst) in enumerate(((exp_s, exp_ref), (count_s, count_ref))):
-        copies.append(pltpu.make_async_copy(src, dst, sems.at[3 + n]))
-        copies[-1].start()
     for copy in copies:
         copy.wait()
 
@@ -374,10 +375,11 @@
             pltpu.VMEM((1, share_cols), jnp.float32),
             pltpu.VMEM((1, blocks), jnp.float32),
             pltpu.VMEM((1, share_cols), jnp.float32),
-            pltpu.VMEM((1, 2 * LANES), jnp.int32),
+            pltpu.SMEM((1,), jnp.int32),
+            pltpu.SMEM((1,), jnp.int32),
         ),
         in_specs=[vmem, vmem, vmem, any_space],
-        out_specs=(vmem, vmem, vmem, vmem),
+        out_specs=(vmem, vmem, vmem, smem, smem),
         scratch_shapes=[
             pltpu.VMEM((1, share_cols), jnp.float32),
             pltpu.VMEM((ROW_GROUP, intra_size, 2, width), jnp.float32),
@@ -389,10 +391,9 @@
             pltpu.SemaphoreType.DMA,
             pltpu.SemaphoreType.DMA,
             pltpu.SemaphoreType.DMA,
+            pltpu.SemaphoreType.DMA((groups,)),
             pltpu.SemaphoreType.DMA,
-            pltpu.SemaphoreType.DMA((groups,)),
-            pltpu.SemaphoreType.DMA((aboves,)),
-            pltpu.SemaphoreType.REGULAR((LINES + intra_size - 2 + aboves,)),
+            pltpu.SemaphoreType.REGULAR((LINES + intra_size - 1,)),
             pltpu.SemaphoreType.REGULAR,
         ],
         compiler_params=pltpu.CompilerParams(collective_id=0, has_side_effects=True),
@@ -407,11 +408,11 @@
             jax.ShapeDtypeStruct((1,), jnp.int32),
             jax.ShapeDtypeStruct((1,), jnp.int32),
         ),
-        in_specs=[vmem] * 4,
+        in_specs=[vmem, vmem, vmem, smem, smem],
         out_specs=(any_space,) * 5,
-        scratch_shapes=[pltpu.SMEM((1,), jnp.int32), pltpu.SMEM((1,), jnp.int32), pltpu.SemaphoreType.DMA((5,))],
+        scratch_shapes=[pltpu.SemaphoreType.DMA((5,))],
         name="finish",
-    )(*(in_vmem(result) for result in results))
+    )(*(in_vmem(result) for result in results[:3]), *results[3:])
     return grad_out, block_scale, master_out, new_exponent.reshape(()), count.reshape(())
 
 

time: 12.2 us -> 12.1 us (level)
    pallas_call x1, Pallas kernels: 9.36 us -> 9.24 us  [on_device(): pl.pallas_call(functools.partial(exchange, inter_size, intra_size, block_...]
where the time goes in v4:
time: 12.1 us; the launch traced here: 11.9 us
  Pallas kernels  9.92 us (82%)
  between operations  2.01 us (17%)
    pallas_call x1, Pallas kernels, on_device(): pl.pallas_call(functools.partial(exchange, inter_size, intra_size, block_...  9.24 us
    pallas_call x1, Pallas kernels, on_device(): pl.pallas_call(finish, out_shape=(jax.ShapeDtypeStruct((1, share_cols), j...  0.67 us

profile of v4, /device:TPU:0, one launch (start us, length us, event | category | flops | bytes accessed | tf_op | source)
XLA Modules:
  0.0 11.9 jit_solution(6543002940007731896)
XLA Ops:
  0.6 0.0 copy-start.1
  0.6 0.0 copy-start
  2.0 0.0 copy-done.1
  2.0 0.0 copy-done
  2.0 9.2 %exchange.1 = (f32[1,2560]{1,0:T(1,128)S(1)}, f32[1,10]{1,0:T(1,128)S(1)}, f32[1,2560]{1,0:T(1,128)S(1)}, s32[1]{0:T(128)S(4)}, s32[1]{0:T(128)S(4)}) custom-call(bf16[1,16,5120]{2,1,0:T(8,128)(2,1)S(1)} %copy-done, f32[1,16,128]{2,1,0:T(8,128)S(1)} %pass_scales.1.s_ref, s32[1,128]{1,0:T(1,128)S(1)} %gather_scalars.1.meta_ref, f32[1,2560]{1,0:T(1,128)} %w_hbm.1), custom_call_target="tpu_custom_call" | custom-call | tf_op jit(solution)/shard_map/exchange/pallas_call | solution.py:372
  11.3 0.7 %finish.1 = (f32[1,2560]{1,0:T(1,128)}, f32[1,10]{1,0:T(1,128)}, f32[1,2560]{1,0:T(1,128)}, s32[1]{0:T(128)}, s32[1]{0:T(128)}) custom-call(f32[1,2560]{1,0:T(1,128)S(1)} %get-tuple-element.15.refs_0_, f32[1,10]{1,0:T(1,128)S(1)} %get-tuple-element.16.refs_1_, f32[1,2560]{1,0:T(1,128)S(1)} %get-tuple-element.17.refs_2_, s32[1]{0:T(128)S(4)} %get-tuple-element.18.refs_3_, ...), custom_call_target="tpu_custom_call" | custom-call | tf_op jit(solution)/shard_map/finish/pallas_call | solution.py:402
  (2 shorter events, 0.0 us)
Async XLA Ops:
  0.6 1.4 %copy-start.1 = (bf16[1,16,20]{2,1,0:T(8,128)(2,1)S(1)}, bf16[1,16,20]{2,1,0:T(8,128)(2,1)}, u32[]{:S(2)}) copy-start(bf16[1,16,20]{2,1,0:T(8,128)(2,1)} %s_ref.1) | copy-start | bytes 1924
  0.6 1.4 %copy-start = (bf16[1,16,5120]{2,1,0:T(8,128)(2,1)S(1)}, bf16[1,16,5120]{2,1,0:T(8,128)(2,1)}, u32[]{:S(2)}) copy-start(bf16[1,16,5120]{2,1,0:T(8,128)(2,1)} %x_ref.1) | copy-start | bytes 491524

commit v5 on v4

--- a/solution.py
+++ b/solution.py
@@ -23,7 +23,7 @@
     return layers, layers * CORES * LINES == inter_size and 1 < layers <= MOST_LAYERS
 
 
-def exchange(inter_size, intra_size, block_len, x_ref, s_ref, meta_ref, w_hbm,
+def exchange(inter_size, intra_size, block_len, x_ref, s_ref, meta_ref, power_ref, w_hbm,
              grad_ref, scale_ref, master_ref, exp_ref, count_ref,
              w_ref, staged, outgoing, incoming, layer_in, layer_sum, sum_in,
              load_sem, send_sem, sum_send_sem, recv_sems, layer_sem, told_sem, mate_sem):
@@ -83,7 +83,7 @@
                 for core in range(KEEPER):
                     pl.when(at_first)(functools.partial(signal, barrier, inter_of(z, y, core), x))
 
-        each_chip(place, ends, greet)
+        each_chip(place, ends, lambda z, y, x: greet(*(lo + hi - 1 - at for lo, hi, at in zip(place, ends, (z, y, x)))))
         pl.when(my_core != KEEPER)(lambda: signal(barrier, inter_of(place[0], place[1], KEEPER), my_intra))
         for core in range(KEEPER):
             pl.when(at_first & (my_core == KEEPER))(
@@ -96,7 +96,8 @@
 
     flag = meta_ref[0:1, 0:1].astype(jnp.float32)
     lane = lax.broadcasted_iota(jnp.int32, (ROW_GROUP, TAIL), 1)
-    flags = jnp.where(lane == scale_lanes, flag, 0.0)
+    power = power_ref[0:1, 0:1].astype(jnp.float32)
+    flags = jnp.where(lane == scale_lanes, flag, jnp.where(lane == scale_lanes + 1, power, 0.0))
 
     def stage(group, shares):
         rows = pl.ds(pl.multiple_of(group * ROW_GROUP, ROW_GROUP), ROW_GROUP)
@@ -216,8 +217,6 @@
             send(target // intra_size, lax.rem(target, intra_size), 0)
 
     incoming[me] = outgoing[my_inter, my_intra]
-    exponent = meta_ref[0:1, 1:2]
-    unscale = jnp.exp2(jnp.broadcast_to(-exponent.astype(jnp.float32), (1, LANES)))
     load.wait()
 
     def add(ref, sources, sums):
@@ -235,6 +234,12 @@
 
     sums = tuple(jnp.zeros((2, LANES), jnp.float32) for _ in range(tiles)) + (jnp.zeros((2, TAIL), jnp.float32),)
     none = sums
+
+    def power_of(sums):
+        lane = lax.broadcasted_iota(jnp.int32, (1, TAIL), 1)
+        power = jnp.sum(jnp.where(lane == scale_lanes + 1, sums[tiles][0:1], 0.0), axis=1, keepdims=True)
+        return power, jnp.exp2(-jnp.broadcast_to(power, (1, LANES)))
+
     if ordered:
         for layer in range(layers - 1):
             @pl.when(place[0] == layer)
@@ -260,6 +265,7 @@
 
         landed(incoming.at[pl.ds(0, per_layer - 1)], recv_sems.at[0])
         sums = add(incoming, pl.ds(place[0] * per_layer, per_layer), sums)
+        near = power_of(sums)
         for group in range(1, layers):
             def direct(sums, group=group):
                 landed(incoming.at[pl.ds(0, per_layer)], recv_sems.at[group])
@@ -275,6 +281,10 @@
         landed(incoming.at[pl.ds(0, total - 1)], recv_sems.at[0])
         sums = lax.fori_loop(
             0, total // SOURCE_GROUP, lambda n, sums: add(incoming, pl.ds(n * SOURCE_GROUP, SOURCE_GROUP), sums), sums)
+    if ordered:
+        power, unscale = lax.cond(place[0] == 0, lambda: near, lambda: power_of(sums))
+    else:
+        power, unscale = power_of(sums)
     lane = lax.broadcasted_iota(jnp.int32, (1, TAIL), 1)
     count = jnp.sum(jnp.where(lane == scale_lanes, sums[tiles][0:1], 0.0), axis=1, keepdims=True).astype(jnp.int32)
     keep = jnp.broadcast_to(count, (1, LANES)) == 0
@@ -301,7 +311,7 @@
         largest = jnp.where(block_lane == n, top, largest)
     scale_ref[...] = largest / 127.0
     total_count = count[0, 0]
-    exp_ref[0] = exponent[0, 0] - jnp.where(total_count > 0, 1, 0)
+    exp_ref[0] = power.astype(jnp.int32)[0, 0] - jnp.where(total_count > 0, 1, 0)
     count_ref[0] = total_count
 
     def sent(layer):
@@ -317,12 +327,12 @@
         landed(incoming.at[pl.ds(0, total - 1)], send_sem)
 
 
-def gather_scalars(pos_ref, exp_ref, meta_ref):
-    lane = lax.broadcasted_iota(jnp.int32, (1, LANES), 1)
-    meta_ref[...] = jnp.where(lane == 0, jnp.where(pos_ref[0, 0] >= 0, 1, 0), exp_ref[...])
-
-
-def pass_scales(meta_ref, s_ref, passed_ref):
+def gather_scalars(pos_ref, meta_ref):
+    meta_ref[...] = jnp.full((1, LANES), jnp.where(pos_ref[0, 0] >= 0, 1, 0), jnp.int32)
+
+
+def pass_scales(meta_ref, s_ref, passed_ref, nothing_ref):
+    nothing_ref[...] = jnp.zeros_like(nothing_ref)
     passed_ref[0, :, pl.ds(0, s_ref.shape[2])] = s_ref[0].astype(jnp.float32)
 
 
@@ -356,19 +366,26 @@
     meta = pl.pallas_call(
         gather_scalars,
         out_shape=pltpu.VMEM((1, LANES), jnp.int32),
-        in_specs=[smem, smem],
+        in_specs=[smem],
         out_specs=vmem,
         cost_estimate=pl.CostEstimate(flops=1000000, bytes_accessed=0, transcendentals=0),
         name="gather_scalars",
-    )(overflow_pos, exponent)
-    passed = pl.pallas_call(
+    )(overflow_pos)
+    passed, nothing = pl.pallas_call(
         pass_scales,
-        out_shape=pltpu.VMEM((1, row_total, LANES), jnp.float32),
+        out_shape=(pltpu.VMEM((1, row_total, LANES), jnp.float32), pltpu.VMEM((1, LANES), jnp.int32)),
         in_specs=[vmem, vmem],
-        out_specs=vmem,
-        cost_estimate=pl.CostEstimate(flops=60000000, bytes_accessed=0, transcendentals=0),
+        out_specs=(vmem, vmem),
+        cost_estimate=pl.CostEstimate(flops=79500000, bytes_accessed=0, transcendentals=0),
         name="pass_scales",
     )(in_vmem(meta), in_vmem(scales))
+    power = lax.cond(
+        lax.axis_index("inter") + lax.axis_index("intra") == 0,
+        lambda exponent, nothing: nothing + exponent,
+        lambda exponent, nothing: nothing,
+        exponent,
+        nothing,
+    )
     results = pl.pallas_call(
         functools.partial(exchange, inter_size, intra_size, block_len),
         out_shape=(
@@ -378,7 +395,7 @@
             pltpu.SMEM((1,), jnp.int32),
             pltpu.SMEM((1,), jnp.int32),
         ),
-        in_specs=[vmem, vmem, vmem, any_space],
+        in_specs=[vmem, vmem, vmem, vmem, any_space],
         out_specs=(vmem, vmem, vmem, smem, smem),
         scratch_shapes=[
             pltpu.VMEM((1, share_cols), jnp.float32),
@@ -398,7 +415,7 @@
         ],
         compiler_params=pltpu.CompilerParams(collective_id=0, has_side_effects=True),
         name="exchange",
-    )(in_vmem(partials), in_vmem(passed), in_vmem(meta), weights)
+    )(in_vmem(partials), in_vmem(passed), in_vmem(meta), in_vmem(power), weights)
     grad_out, block_scale, master_out, new_exponent, count = pl.pallas_call(
         finish,
         out_shape=(

time: 12.1 us -> 11.7 us (0.967)
  the two profiles are of different devices: /device:TPU:0 before, /device:TPU:8 now
where the time goes in v5:
time: 11.7 us; the launch traced here: 11.5 us
  Pallas kernels  9.88 us (84%)
  between operations  1.38 us (12%)
  local copies, waits for them, and re-layouts  0.2 us (2%)
    pallas_call x1, Pallas kernels, on_device(): pl.pallas_call(functools.partial(exchange, inter_size, intra_size, block_...  9.2 us
    pallas_call x1, Pallas kernels, on_device(): pl.pallas_call(finish, out_shape=(jax.ShapeDtypeStruct((1, share_cols), j...  0.67 us

profile of v5, /device:TPU:8, one launch (start us, length us, event | category | flops | bytes accessed | tf_op | source)
XLA Modules:
  0.0 11.5 jit_solution(17114063775594103992)
XLA Ops:
  0.6 0.0 copy-start.1
  0.6 0.0 copy-start
  1.4 0.0 copy-done.1
  1.4 0.2 %copy-done = bf16[1,16,5120]{2,1,0:T(8,128)(2,1)S(1)} copy-done((bf16[1,16,5120]{2,1,0:T(8,128)(2,1)S(1)}, bf16[1,16,5120]{2,1,0:T(8,128)(2,1)}, u32[]{:S(2)}) %copy-start) | copy-done | bytes 163864
  1.6 9.2 %exchange.1 = (f32[1,2560]{1,0:T(1,128)S(1)}, f32[1,10]{1,0:T(1,128)S(1)}, f32[1,2560]{1,0:T(1,128)S(1)}, s32[1]{0:T(128)S(4)}, s32[1]{0:T(128)S(4)}) custom-call(bf16[1,16,5120]{2,1,0:T(8,128)(2,1)S(1)} %copy-done, f32[1,16,128]{2,1,0:T(8,128)S(1)} %get-tuple-element.27.s_ref, s32[1,128]{1,0:T(1,128)S(1)} %gather_scalars.1.meta_ref, ...), custom_call_target="tpu_custom_call" | custom-call | tf_op jit(solution)/shard_map/exchange/pallas_call | solution.py:389
  10.8 0.7 %finish.1 = (f32[1,2560]{1,0:T(1,128)}, f32[1,10]{1,0:T(1,128)}, f32[1,2560]{1,0:T(1,128)}, s32[1]{0:T(128)}, s32[1]{0:T(128)}) custom-call(f32[1,2560]{1,0:T(1,128)S(1)} %get-tuple-element.29.refs_0_, f32[1,10]{1,0:T(1,128)S(1)} %get-tuple-element.30.refs_1_, f32[1,2560]{1,0:T(1,128)S(1)} %get-tuple-element.31.refs_2_, s32[1]{0:T(128)S(4)} %get-tuple-element.32.refs_3_, ...), custom_call_target="tpu_custom_call" | custom-call | tf_op jit(solution)/shard_map/finish/pallas_call | solution.py:419
  (3 shorter events, 0.0 us)
Async XLA Ops:
  0.6 0.7 %copy-start.1 = (bf16[1,16,20]{2,1,0:T(8,128)(2,1)S(1)}, bf16[1,16,20]{2,1,0:T(8,128)(2,1)}, u32[]{:S(2)}) copy-start(bf16[1,16,20]{2,1,0:T(8,128)(2,1)} %s_ref.1) | copy-start | bytes 1924
  0.6 0.9 %copy-start = (bf16[1,16,5120]{2,1,0:T(8,128)(2,1)S(1)}, bf16[1,16,5120]{2,1,0:T(8,128)(2,1)}, u32[]{:S(2)}) copy-start(bf16[1,16,5120]{2,1,0:T(8,128)(2,1)} %x_ref.1) | copy-start | bytes 491524

commit v6 on v5

--- a/solution.py
+++ b/solution.py
@@ -266,23 +266,29 @@
         landed(incoming.at[pl.ds(0, per_layer - 1)], recv_sems.at[0])
         sums = add(incoming, pl.ds(place[0] * per_layer, per_layer), sums)
         near = power_of(sums)
-        for group in range(1, layers):
+        others = [layers - 1, *range(1, layers - 1)]
+        for group, other in enumerate(others, 1):
             def direct(sums, group=group):
                 landed(incoming.at[pl.ds(0, per_layer)], recv_sems.at[group])
                 return add(incoming, pl.ds((place[0] + group) * per_layer, per_layer), sums)
 
-            def summed(sums, group=group):
+            def summed(sums, group=other):
                 below = sum_in.at[layers - group - 1]
                 landed(below, recv_sems.at[group])
                 return tuple(each + below[:, pl.ds(t * LANES, each.shape[1])] for t, each in enumerate(sums))
 
-            sums = lax.cond(place[0] + group < layers, direct, summed, sums)
+            def upper(sums, other=other, direct=direct, summed=summed):
+                return lax.cond(place[0] + other < layers, functools.partial(direct, group=other), summed, sums)
+
+            sums = lax.cond(place[0] == 0, direct, upper, sums)
+            if group == 1:
+                near = lax.cond(place[0] == 0, lambda near: near, lambda near: power_of(sums), near)
     else:
         landed(incoming.at[pl.ds(0, total - 1)], recv_sems.at[0])
         sums = lax.fori_loop(
             0, total // SOURCE_GROUP, lambda n, sums: add(incoming, pl.ds(n * SOURCE_GROUP, SOURCE_GROUP), sums), sums)
     if ordered:
-        power, unscale = lax.cond(place[0] == 0, lambda: near, lambda: power_of(sums))
+        power, unscale = lax.cond(place[0] < 2, lambda: near, lambda: power_of(sums))
     else:
         power, unscale = power_of(sums)
     lane = lax.broadcasted_iota(jnp.int32, (1, TAIL), 1)

time: 11.7 us -> 11.6 us (level)
  the two profiles are of different devices: /device:TPU:8 before, /device:TPU:0 now
where the time goes in v6:
time: 11.6 us; the launch traced here: 11.4 us
  Pallas kernels  9.37 us (81%)
  between operations  1.38 us (12%)
  other arithmetic  0.66 us (6%)
    pallas_call x1, Pallas kernels, on_device(): pl.pallas_call(functools.partial(exchange, inter_size, intra_size, block_...  8.69 us
    pallas_call x1, Pallas kernels, on_device(): pl.pallas_call(finish, out_shape=(jax.ShapeDtypeStruct((1, share_cols), j...  0.67 us
    add x1, other arithmetic, on_device(): nothing + exponent  0.66 us

profile of v6, /device:TPU:0, one launch (start us, length us, event | category | flops | bytes accessed | tf_op | source)
XLA Modules:
  0.0 11.4 jit_solution(4305213382257663459)
XLA Ops:
  0.6 0.0 copy-start.1
  0.6 0.0 copy-start
  1.4 0.0 copy-done.1
  1.4 0.7 %conditional.1 = (s32[1,128]{1,0:T(1,128)S(1)}) conditional(s32[]{:T(128)} %convert_element_type.3, s32[1,128]{1,0:T(1,128)S(1)} %get-tuple-element.28, (s32[]{:T(128)}, s32[1,128]{1,0:T(1,128)S(1)}) %tuple.14), branch_computations={%region_0.0_spmd, %region_1.0_spmd} | conditional | flops 128 | bytes 1036 | solution.py:388
  1.4 0.7 %broadcast_add_fusion = s32[1,128]{1,0:T(1,128)S(1)} fusion(s32[1,128]{1,0:T(1,128)S(1)} %get-tuple-element.8, s32[]{:T(128)} %get-tuple-element.40), kind=kLoop, calls=%fused_computation | loop fusion | flops 128 | bytes 1028 | tf_op jit(solution)/shard_map/cond/branch_1_fun/add | solution.py:390
  2.1 0.0 copy-done
  2.1 8.7 %exchange.1 = (f32[1,2560]{1,0:T(1,128)S(1)}, f32[1,10]{1,0:T(1,128)S(1)}, f32[1,2560]{1,0:T(1,128)S(1)}, s32[1]{0:T(128)S(4)}, s32[1]{0:T(128)S(4)}) custom-call(bf16[1,16,5120]{2,1,0:T(8,128)(2,1)S(1)} %copy-done, f32[1,16,128]{2,1,0:T(8,128)S(1)} %get-tuple-element.27.s_ref, s32[1,128]{1,0:T(1,128)S(1)} %gather_scalars.1.meta_ref, ...), custom_call_target="tpu_custom_call" | custom-call | tf_op jit(solution)/shard_map/exchange/pallas_call | solution.py:395
  10.8 0.7 %finish.1 = (f32[1,2560]{1,0:T(1,128)}, f32[1,10]{1,0:T(1,128)}, f32[1,2560]{1,0:T(1,128)}, s32[1]{0:T(128)}, s32[1]{0:T(128)}) custom-call(f32[1,2560]{1,0:T(1,128)S(1)} %get-tuple-element.29.refs_0_, f32[1,10]{1,0:T(1,128)S(1)} %get-tuple-element.30.refs_1_, f32[1,2560]{1,0:T(1,128)S(1)} %get-tuple-element.31.refs_2_, s32[1]{0:T(128)S(4)} %get-tuple-element.32.refs_3_, ...), custom_call_target="tpu_custom_call" | custom-call | tf_op jit(solution)/shard_map/finish/pallas_call | solution.py:425
  (2 shorter events, 0.0 us)
Async XLA Ops:
  0.6 0.7 %copy-start.1 = (bf16[1,16,20]{2,1,0:T(8,128)(2,1)S(1)}, bf16[1,16,20]{2,1,0:T(8,128)(2,1)}, u32[]{:S(2)}) copy-start(bf16[1,16,20]{2,1,0:T(8,128)(2,1)} %s_ref.1) | copy-start | bytes 1924
  0.6 1.4 %copy-start = (bf16[1,16,5120]{2,1,0:T(8,128)(2,1)S(1)}, bf16[1,16,5120]{2,1,0:T(8,128)(2,1)}, u32[]{:S(2)}) copy-start(bf16[1,16,5120]{2,1,0:T(8,128)(2,1)} %x_ref.1) | copy-start | bytes 491524

commit v7 on v6

--- a/solution.py
+++ b/solution.py
@@ -345,7 +345,7 @@
 def finish(*refs):
     half = (len(refs) - 1) // 2
     copies = [pltpu.make_async_copy(src, dst, refs[-1].at[n]) for n, (src, dst) in enumerate(zip(refs[:half], refs[half:-1]))]
-    for copy in copies:
+    for copy in reversed(copies):
         copy.start()
     for copy in copies:
         copy.wait()

time: 11.6 us -> 11.6 us (level)
  no operation moved by 1% of the time
where the time goes in v7:
time: 11.6 us; the launch traced here: 11.4 us
  Pallas kernels  9.37 us (81%)
  between operations  1.38 us (12%)
  other arithmetic  0.66 us (6%)
    pallas_call x1, Pallas kernels, on_device(): pl.pallas_call(functools.partial(exchange, inter_size, intra_size, block_...  8.69 us
    pallas_call x1, Pallas kernels, on_device(): pl.pallas_call(finish, out_shape=(jax.ShapeDtypeStruct((1, share_cols), j...  0.68 us
    add x1, other arithmetic, on_device(): nothing + exponent  0.66 us

profile of v7, /device:TPU:0, one launch (start us, length us, event | category | flops | bytes accessed | tf_op | source)
XLA Modules:
  0.0 11.4 jit_solution(8391870300779191643)
XLA Ops:
  0.6 0.0 copy-start.1
  0.6 0.0 copy-start
  1.4 0.0 copy-done.1
  1.4 0.7 %conditional.1 = (s32[1,128]{1,0:T(1,128)S(1)}) conditional(s32[]{:T(128)} %convert_element_type.3, s32[1,128]{1,0:T(1,128)S(1)} %get-tuple-element.28, (s32[]{:T(128)}, s32[1,128]{1,0:T(1,128)S(1)}) %tuple.14), branch_computations={%region_0.0_spmd, %region_1.0_spmd} | conditional | flops 128 | bytes 1036 | solution.py:388
  1.4 0.7 %broadcast_add_fusion = s32[1,128]{1,0:T(1,128)S(1)} fusion(s32[1,128]{1,0:T(1,128)S(1)} %get-tuple-element.8, s32[]{:T(128)} %get-tuple-element.40), kind=kLoop, calls=%fused_computation | loop fusion | flops 128 | bytes 1028 | tf_op jit(solution)/shard_map/cond/branch_1_fun/add | solution.py:390
  2.1 0.0 copy-done
  2.1 8.7 %exchange.1 = (f32[1,2560]{1,0:T(1,128)S(1)}, f32[1,10]{1,0:T(1,128)S(1)}, f32[1,2560]{1,0:T(1,128)S(1)}, s32[1]{0:T(128)S(4)}, s32[1]{0:T(128)S(4)}) custom-call(bf16[1,16,5120]{2,1,0:T(8,128)(2,1)S(1)} %copy-done, f32[1,16,128]{2,1,0:T(8,128)S(1)} %get-tuple-element.27.s_ref, s32[1,128]{1,0:T(1,128)S(1)} %gather_scalars.1.meta_ref, ...), custom_call_target="tpu_custom_call" | custom-call | tf_op jit(solution)/shard_map/exchange/pallas_call | solution.py:395
  10.8 0.7 %finish.1 = (f32[1,2560]{1,0:T(1,128)}, f32[1,10]{1,0:T(1,128)}, f32[1,2560]{1,0:T(1,128)}, s32[1]{0:T(128)}, s32[1]{0:T(128)}) custom-call(f32[1,2560]{1,0:T(1,128)S(1)} %get-tuple-element.29.refs_0_, f32[1,10]{1,0:T(1,128)S(1)} %get-tuple-element.30.refs_1_, f32[1,2560]{1,0:T(1,128)S(1)} %get-tuple-element.31.refs_2_, s32[1]{0:T(128)S(4)} %get-tuple-element.32.refs_3_, ...), custom_call_target="tpu_custom_call" | custom-call | tf_op jit(solution)/shard_map/finish/pallas_call | solution.py:425
  (2 shorter events, 0.0 us)
Async XLA Ops:
  0.6 0.7 %copy-start.1 = (bf16[1,16,20]{2,1,0:T(8,128)(2,1)S(1)}, bf16[1,16,20]{2,1,0:T(8,128)(2,1)}, u32[]{:S(2)}) copy-start(bf16[1,16,20]{2,1,0:T(8,128)(2,1)} %s_ref.1) | copy-start | bytes 1924
  0.6 1.4 %copy-start = (bf16[1,16,5120]{2,1,0:T(8,128)(2,1)S(1)}, bf16[1,16,5120]{2,1,0:T(8,128)(2,1)}, u32[]{:S(2)}) copy-start(bf16[1,16,5120]{2,1,0:T(8,128)(2,1)} %x_ref.1) | copy-start | bytes 491524
